TPU v7x, 32 devices: a whole 2x2x4 slice. The times are simulated.
32 devices in a mesh: pb: 8 (over z, core), sp: 4 (over y, x).
Axes of the slice: x: 2, y: 2, z: 4, core: 2. Of those that a mesh axis runs over, the one named last changes fastest.
Arguments:
- nodes: bfloat16 [8192, 1024], P(('pb', 'sp')), may hold values from -40 to 40
- project_in: bfloat16 [1024, 3072], replicated, may hold values from -0.3 to 0.3
- project_out: bfloat16 [1024, 1024], replicated, may hold values from -0.1875 to 0.1875
- tile_list: int32 [64, 32], replicated, may hold values from 0 to 63, as said below
- tile_count: int32 [64], replicated, may hold values from 2 to 32, as said below
Outputs:
- mixed: bfloat16 [8192, 1024], P(('pb', 'sp'))
Inputs may be any that keep to these rules, and one draw needn't show every extreme that they name: `tile_list`: position 0 of row t is t itself. Over the live positions of the rows of one group (rows g * 8 to (g + 1) * 8 - 1), at most 4 distinct tiles of any other group are listed, and exactly 4 of the next group's tiles (group g + 1, after the last comes the first). A tile may stand more than once in a row. `tile_count`: row 0 has 32.
All inputs are finite; a program needn't handle non-finite values.
Results may differ from a plain program's by a relative error of at most 0.0082.
Values may be sent and summed in bfloat16 or wider, within the bound.
A program may use at most 128 MiB of HBM per device.

v0:
```python
import jax
import jax.numpy as jnp
from jax import lax
from jax.sharding import PartitionSpec as P

HEADS = 16
HEAD_DIM = 64
TILE = 128


NEGATIVE = -1e30
per_block = 8


def live_mask(tile_list, tile_count):
    listed = tile_list.shape[1]
    places = jnp.arange(listed, dtype=jnp.int32)
    inside = places[None, :] < tile_count[:, None]
    earlier = (places[:, None] > places[None, :])[None, :, :]
    repeats = (tile_list[:, :, None] == tile_list[:, None, :]) & earlier
    return inside & jnp.logical_not(jnp.any(repeats, axis=2))


def attend(queries, key_table, value_table, tile_index, usable, blocks):
    group_tiles, heads_here, tile_len, head_dim = queries.shape
    score_scale = head_dim ** (-0.5)

    def advance(block_index, state_now):
        highest, running_total, gathered = state_now
        chosen = lax.dynamic_slice_in_dim(tile_index, block_index * per_block, per_block, 1)
        allowed = lax.dynamic_slice_in_dim(usable, block_index * per_block, per_block, 1)
        fetched_keys = key_table[chosen]
        fetched_values = value_table[chosen]
        scores = (
            jnp.einsum(
                "qhbe,qjhek->qhbjk", queries, fetched_keys, preferred_element_type=jnp.float32
            )
            * score_scale
        )
        allowed_mask = allowed[:, None, None, :, None]
        scores = jnp.where(allowed_mask, scores, NEGATIVE)
        raised = jnp.maximum(highest, jnp.max(scores, axis=(3, 4)))
        weights = jnp.where(allowed_mask, jnp.exp(scores - raised[..., None, None]), 0.0)
        fade_factor = jnp.exp(highest - raised)
        running_total = running_total * fade_factor + jnp.sum(weights, axis=(3, 4))
        gathered = gathered * fade_factor[..., None] + jnp.einsum(
            "qhbjk,qjhke->qhbe",
            weights.astype(jnp.bfloat16),
            fetched_values,
            preferred_element_type=jnp.float32,
        )
        return (raised, running_total, gathered)

    start_state = (
        jnp.full((group_tiles, heads_here, tile_len), NEGATIVE, jnp.float32),
        jnp.zeros((group_tiles, heads_here, tile_len), jnp.float32),
        jnp.zeros((group_tiles, heads_here, tile_len, head_dim), jnp.float32),
    )
    highest, running_total, gathered = lax.fori_loop(0, blocks, advance, start_state)
    return gathered / running_total[..., None]


def shards(nodes, project_in, project_out, tile_list, tile_count):
    node_rows = nodes.shape[0]
    sp_count = lax.axis_size("sp")
    heads_here = HEADS // sp_count
    group_tiles = node_rows * sp_count // TILE
    projected = jnp.dot(nodes, project_in, preferred_element_type=jnp.float32).astype(jnp.bfloat16)
    projected = projected.reshape(node_rows, HEADS, 3 * HEAD_DIM)
    regrouped = lax.all_to_all(projected, "sp", split_axis=1, concat_axis=0, tiled=True)
    regrouped = regrouped.reshape(group_tiles, TILE, heads_here, 3 * HEAD_DIM).transpose(0, 2, 1, 3)
    queries = regrouped[..., :HEAD_DIM]
    key_local = jnp.swapaxes(regrouped[..., HEAD_DIM : 2 * HEAD_DIM], 2, 3)
    value_local = regrouped[..., 2 * HEAD_DIM :]
    pb_index = lax.axis_index("pb")
    usable_all = live_mask(tile_list, tile_count)
    first_tile = pb_index * group_tiles
    my_list = lax.dynamic_slice_in_dim(tile_list, first_tile, group_tiles, 0)
    my_usable = lax.dynamic_slice_in_dim(usable_all, first_tile, group_tiles, 0)
    my_counts = lax.dynamic_slice_in_dim(tile_count, first_tile, group_tiles, 0)
    blocks = (jnp.max(my_counts) + per_block - 1) // per_block
    key_table, value_table = (
        lax.all_gather(key_local, "pb", axis=0, tiled=True),
        lax.all_gather(value_local, "pb", axis=0, tiled=True),
    )
    attended = attend(queries, key_table, value_table, my_list, my_usable, blocks)
    attended = (
        attended.astype(jnp.bfloat16)
        .transpose(0, 2, 1, 3)
        .reshape(group_tiles * TILE, heads_here * HEAD_DIM)
    )
    joined = lax.all_to_all(attended, "sp", split_axis=0, concat_axis=1, tiled=True)
    mixed_out = nodes.astype(jnp.float32) + jnp.dot(
        joined, project_out, preferred_element_type=jnp.float32
    )
    return mixed_out.astype(jnp.bfloat16)


def solution(mesh):
    in_specs = (P(("pb", "sp"), None), P(), P(), P(), P())
    out_specs = P(("pb", "sp"), None)
    return jax.shard_map(shards, mesh=mesh, in_specs=in_specs, out_specs=out_specs, check_vma=False)
```

profile of v0, /device:TPU:0, one launch (start us, length us, event | category | flops | bytes accessed | tf_op | source)
XLA Modules:
  0.0 321.5 jit_solution(13701120549022610489)
XLA Ops:
  6.5 6.1 %convolution_convert_fusion = bf16[256,3072]{1,0:T(8,128)(2,1)} fusion(bf16[256,1024]{1,0:T(8,128)(2,1)} %param.7, bf16[1024,3072]{1,0:T(8,128)(2,1)} %param.8), kind=kOutput, calls=%fused_computation.30 | convolution fusion | flops 1611399168 | bytes 8388608 | tf_op jit(solution)/shard_map/dot_general | solution.py:68
  12.6 2.6 copy.44
  15.2 24.9 %all_to_all.34 = bf16[256,16,192]{0,2,1:T(8,128)(2,1)S(1)} all-to-all(bf16[256,16,192]{0,2,1:T(8,128)(2,1)} %bitcast.88), channel_id=1, replica_groups=mesh['pb'=8,'sp'=4] {'sp'}, dimensions={1} | all-to-all | bytes 3145728 | tf_op jit(solution)/shard_map/all_to_all | solution.py:70
  40.2 2.4 copy.45
  42.5 3.6 %reshape.32 = bf16[8,128,4,192]{1,0,3,2:T(8,128)(2,1)} reshape(bf16[4,256,4,192]{1,0,3,2:T(4,128)(2,1)} %copy.45) | data formatting | bytes 3145728 | tf_op jit(solution)/shard_map/reshape | solution.py:71
  46.2 2.4 fusion.32
  48.6 0.0 all-gather.5.cloned.1.call-update
  48.6 0.0 all-gather.3.cloned.1.call-start
  48.7 0.7 all-gather.3.cloned.1.call-update
  49.4 0.7 fusion.31
  50.7 0.0 copy-done.2
  50.7 0.1 constant_dynamic-slice_fusion.2
  50.8 0.2 and_reduce_fusion
  51.0 0.1 fusion.30
  51.1 0.9 copy.48
  52.0 44.4 %all-gather.5.cloned.1.call-done = bf16[64,4,128,64]{2,0,3,1:T(8,128)(2,1)} async-done(((bf16[8,4,128,64]{2,0,3,1:T(8,128)(2,1)}), bf16[64,4,128,64]{2,0,3,1:T(8,128)(2,1)}) %all-gather.5.cloned.1.call-update) | async-done | bytes 4194320 | tf_op jit(solution)/shard_map/all_gather | solution.py:84
  96.4 8.8 %copy.49 = bf16[64,4,128,64]{3,2,1,0:T(8,128)(2,1)} copy(bf16[64,4,128,64]{2,0,3,1:T(8,128)(2,1)} %all-gather.5.cloned.1.call-done) | data formatting | bytes 8388608 | tf_op jit(solution)/shard_map/while | solution.py:59
  105.3 38.8 %all-gather.3.cloned.1.call-done = bf16[64,4,64,128]{3,0,2,1:T(8,128)(2,1)} async-done(((bf16[8,4,64,128]{3,0,2,1:T(8,128)(2,1)}), bf16[64,4,64,128]{3,0,2,1:T(8,128)(2,1)}) %all-gather.3.cloned.1.call-update) | async-done | bytes 4194320 | tf_op jit(solution)/shard_map/all_gather | solution.py:83
  144.1 6.9 %copy.47 = bf16[64,4,64,128]{3,2,1,0:T(8,128)(2,1)} copy(bf16[64,4,64,128]{3,0,2,1:T(8,128)(2,1)} %all-gather.3.cloned.1.call-done) | data formatting | bytes 8388608 | tf_op jit(solution)/shard_map/while | solution.py:59
  151.0 0.1 broadcast_in_dim.46
  151.1 147.7 %while.14 = (s32[]{:T(128)}, f32[8,4,128]{2,1,0:T(4,128)S(1)}, f32[8,4,128]{2,1,0:T(4,128)S(1)}, f32[8,4,128,64]{2,3,1,0:T(8,128)S(1)}, s32[]{:T(128)}, /*index=...) while((s32[]{:T(128)}, f32[8,4,128]{2,1,0:T(4,128)S(1)}, ...), condition=%wide.region_5.6_spmd, body=%wide.region_2.5_spmd.sunk | while | flops 1128801536 | bytes 145497504 | solution.py:59
  151.4 0.1 copy.77
  151.4 0.1 reshape.64
  151.5 5.2 %gather_fusion = bf16[64,4,64,128]{3,2,1,0:T(8,128)(2,1)} fusion(bf16[64,4,64,128]{3,2,1,0:T(8,128)(2,1)} %get-tuple-element.239, s32[1024]{0:T(1024)S(1)} %pad_clamp_fusion.2), kind=kCustom, calls=%fused_computation.clone.1 | custom fusion | bytes 8388864 | tf_op jit(solution)/shard_map/while/body/gather | solution.py:32
  156.7 0.1 copy.76
  156.8 6.1 %bitcast_reduce_fusion.2 = (f32[8,4,128]{2,1,0:T(4,128)S(1)}, f32[8,4,8,128,128]{4,3,2,1,0:T(8,128)S(1)}) fusion(pred[8,8]{1,0:T(8,128)(4,1)S(1)} %copy.76, bf16[8,4,128,64]{2,3,1,0:T(8,128)(2,1)} %get-tuple-element.240, bf16[8,8,4,64,128]{4,3,2,1,0:T(8,128)(2,1)} %bitcast.85), kind=kOutput, calls=%fused_computation.3.clone.1 | convolution fusion | flops 549449728 | bytes 21512256 | tf_op jit(solution)/shard_map/while/body/qhbe,qjhek->qhbjk/dot_general | solution.py:35
  163.0 4.7 %fusion.43 = f32[8,4,128]{2,1,0:T(4,128)S(1)} fusion(f32[8,4,8,128,128]{4,3,2,1,0:T(8,128)S(1)} %get-tuple-element.201, f32[8,4,128]{2,1,0:T(4,128)S(1)} %max.4, pred[8,8]{1,0:T(8,128)(4,1)S(1)} %copy.76), kind=kLoop, calls=%fused_computation.8.clone.1 | loop fusion | flops 20967424 | bytes 16810048 | tf_op jit(solution)/shard_map/while/body/reduce_sum | solution.py:45
  167.7 1.0 copy-done.1
  168.7 8.9 %gather_fusion.1 = bf16[64,4,128,64]{3,2,1,0:T(8,128)(2,1)} fusion(bf16[64,4,128,64]{3,2,1,0:T(8,128)(2,1)} %get-tuple-element.241, s32[1024]{0:T(1024)S(1)} %pad_clamp_fusion.2), kind=kCustom, calls=%fused_computation.1.clone.1 | custom fusion | bytes 8388864 | tf_op jit(solution)/shard_map/while/body/gather | solution.py:33
  177.6 10.6 %fusion.44 = f32[8,4,128,64]{2,3,1,0:T(8,128)S(1)} fusion(bf16[8,8,4,128,64]{4,3,2,1,0:T(8,128)(2,1)} %bitcast.84, f32[8,4,8,128,128]{4,3,2,1,0:T(8,128)} %copy-done.1, f32[8,4,128]{2,1,0:T(4,128)S(1)} %max.4, pred[8,8]{1,0:T(8,128)(4,1)S(1)} %copy.76, f32[8,4,128,64]{2,3,1,0:T(8,128)S(1)} %get-tuple-element.221, f32[8,4,128]{2,1,0:T(4,128)S(1)} %bitcast.95), kind=kOutput, calls=%fused_computation.19.clone.1 | convolution fusion | flops 558366720 | bytes 23101504 | tf_op jit(solution)/shard_map/while/body/qhbjk,qjhke->qhbe/dot_general | solution.py:46
  188.2 0.1 copy.77
  188.3 0.1 reshape.64
  188.4 5.2 %gather_fusion = bf16[64,4,64,128]{3,2,1,0:T(8,128)(2,1)} fusion(bf16[64,4,64,128]{3,2,1,0:T(8,128)(2,1)} %get-tuple-element.239, s32[1024]{0:T(1024)S(1)} %pad_clamp_fusion.2), kind=kCustom, calls=%fused_computation.clone.1 | custom fusion | bytes 8388864 | tf_op jit(solution)/shard_map/while/body/gather | solution.py:32
  193.6 0.1 copy.76
  193.7 6.1 %bitcast_reduce_fusion.2 = (f32[8,4,128]{2,1,0:T(4,128)S(1)}, f32[8,4,8,128,128]{4,3,2,1,0:T(8,128)S(1)}) fusion(pred[8,8]{1,0:T(8,128)(4,1)S(1)} %copy.76, bf16[8,4,128,64]{2,3,1,0:T(8,128)(2,1)} %get-tuple-element.240, bf16[8,8,4,64,128]{4,3,2,1,0:T(8,128)(2,1)} %bitcast.85), kind=kOutput, calls=%fused_computation.3.clone.1 | convolution fusion | flops 549449728 | bytes 21512256 | tf_op jit(solution)/shard_map/while/body/qhbe,qjhek->qhbjk/dot_general | solution.py:35
  199.9 4.7 %fusion.43 = f32[8,4,128]{2,1,0:T(4,128)S(1)} fusion(f32[8,4,8,128,128]{4,3,2,1,0:T(8,128)S(1)} %get-tuple-element.201, f32[8,4,128]{2,1,0:T(4,128)S(1)} %max.4, pred[8,8]{1,0:T(8,128)(4,1)S(1)} %copy.76), kind=kLoop, calls=%fused_computation.8.clone.1 | loop fusion | flops 20967424 | bytes 16810048 | tf_op jit(solution)/shard_map/while/body/reduce_sum | solution.py:45
  204.5 1.0 copy-done.1
  205.6 8.9 %gather_fusion.1 = bf16[64,4,128,64]{3,2,1,0:T(8,128)(2,1)} fusion(bf16[64,4,128,64]{3,2,1,0:T(8,128)(2,1)} %get-tuple-element.241, s32[1024]{0:T(1024)S(1)} %pad_clamp_fusion.2), kind=kCustom, calls=%fused_computation.1.clone.1 | custom fusion | bytes 8388864 | tf_op jit(solution)/shard_map/while/body/gather | solution.py:33
  214.5 10.6 %fusion.44 = f32[8,4,128,64]{2,3,1,0:T(8,128)S(1)} fusion(bf16[8,8,4,128,64]{4,3,2,1,0:T(8,128)(2,1)} %bitcast.84, f32[8,4,8,128,128]{4,3,2,1,0:T(8,128)} %copy-done.1, f32[8,4,128]{2,1,0:T(4,128)S(1)} %max.4, pred[8,8]{1,0:T(8,128)(4,1)S(1)} %copy.76, f32[8,4,128,64]{2,3,1,0:T(8,128)S(1)} %get-tuple-element.221, f32[8,4,128]{2,1,0:T(4,128)S(1)} %bitcast.95), kind=kOutput, calls=%fused_computation.19.clone.1 | convolution fusion | flops 558366720 | bytes 23101504 | tf_op jit(solution)/shard_map/while/body/qhbjk,qjhke->qhbe/dot_general | solution.py:46
  225.1 0.1 copy.77
  225.1 0.1 reshape.64
  225.2 5.2 %gather_fusion = bf16[64,4,64,128]{3,2,1,0:T(8,128)(2,1)} fusion(bf16[64,4,64,128]{3,2,1,0:T(8,128)(2,1)} %get-tuple-element.239, s32[1024]{0:T(1024)S(1)} %pad_clamp_fusion.2), kind=kCustom, calls=%fused_computation.clone.1 | custom fusion | bytes 8388864 | tf_op jit(solution)/shard_map/while/body/gather | solution.py:32
  230.5 0.1 copy.76
  230.5 6.1 %bitcast_reduce_fusion.2 = (f32[8,4,128]{2,1,0:T(4,128)S(1)}, f32[8,4,8,128,128]{4,3,2,1,0:T(8,128)S(1)}) fusion(pred[8,8]{1,0:T(8,128)(4,1)S(1)} %copy.76, bf16[8,4,128,64]{2,3,1,0:T(8,128)(2,1)} %get-tuple-element.240, bf16[8,8,4,64,128]{4,3,2,1,0:T(8,128)(2,1)} %bitcast.85), kind=kOutput, calls=%fused_computation.3.clone.1 | convolution fusion | flops 549449728 | bytes 21512256 | tf_op jit(solution)/shard_map/while/body/qhbe,qjhek->qhbjk/dot_general | solution.py:35
  236.7 0.0 copy-start.1
  236.7 4.7 %fusion.43 = f32[8,4,128]{2,1,0:T(4,128)S(1)} fusion(f32[8,4,8,128,128]{4,3,2,1,0:T(8,128)S(1)} %get-tuple-element.201, f32[8,4,128]{2,1,0:T(4,128)S(1)} %max.4, pred[8,8]{1,0:T(8,128)(4,1)S(1)} %copy.76), kind=kLoop, calls=%fused_computation.8.clone.1 | loop fusion | flops 20967424 | bytes 16810048 | tf_op jit(solution)/shard_map/while/body/reduce_sum | solution.py:45
  241.4 1.0 copy-done.1
  242.4 8.9 %gather_fusion.1 = bf16[64,4,128,64]{3,2,1,0:T(8,128)(2,1)} fusion(bf16[64,4,128,64]{3,2,1,0:T(8,128)(2,1)} %get-tuple-element.241, s32[1024]{0:T(1024)S(1)} %pad_clamp_fusion.2), kind=kCustom, calls=%fused_computation.1.clone.1 | custom fusion | bytes 8388864 | tf_op jit(solution)/shard_map/while/body/gather | solution.py:33
  251.3 10.6 %fusion.44 = f32[8,4,128,64]{2,3,1,0:T(8,128)S(1)} fusion(bf16[8,8,4,128,64]{4,3,2,1,0:T(8,128)(2,1)} %bitcast.84, f32[8,4,8,128,128]{4,3,2,1,0:T(8,128)} %copy-done.1, f32[8,4,128]{2,1,0:T(4,128)S(1)} %max.4, pred[8,8]{1,0:T(8,128)(4,1)S(1)} %copy.76, f32[8,4,128,64]{2,3,1,0:T(8,128)S(1)} %get-tuple-element.221, f32[8,4,128]{2,1,0:T(4,128)S(1)} %bitcast.95), kind=kOutput, calls=%fused_computation.19.clone.1 | convolution fusion | flops 558366720 | bytes 23101504 | tf_op jit(solution)/shard_map/while/body/qhbjk,qjhke->qhbe/dot_general | solution.py:46
  262.0 0.1 copy.77
  262.0 0.1 reshape.64
  262.1 5.2 %gather_fusion = bf16[64,4,64,128]{3,2,1,0:T(8,128)(2,1)} fusion(bf16[64,4,64,128]{3,2,1,0:T(8,128)(2,1)} %get-tuple-element.239, s32[1024]{0:T(1024)S(1)} %pad_clamp_fusion.2), kind=kCustom, calls=%fused_computation.clone.1 | custom fusion | bytes 8388864 | tf_op jit(solution)/shard_map/while/body/gather | solution.py:32
  267.4 0.1 copy.76
  267.4 6.1 %bitcast_reduce_fusion.2 = (f32[8,4,128]{2,1,0:T(4,128)S(1)}, f32[8,4,8,128,128]{4,3,2,1,0:T(8,128)S(1)}) fusion(pred[8,8]{1,0:T(8,128)(4,1)S(1)} %copy.76, bf16[8,4,128,64]{2,3,1,0:T(8,128)(2,1)} %get-tuple-element.240, bf16[8,8,4,64,128]{4,3,2,1,0:T(8,128)(2,1)} %bitcast.85), kind=kOutput, calls=%fused_computation.3.clone.1 | convolution fusion | flops 549449728 | bytes 21512256 | tf_op jit(solution)/shard_map/while/body/qhbe,qjhek->qhbjk/dot_general | solution.py:35
  273.6 4.7 %fusion.43 = f32[8,4,128]{2,1,0:T(4,128)S(1)} fusion(f32[8,4,8,128,128]{4,3,2,1,0:T(8,128)S(1)} %get-tuple-element.201, f32[8,4,128]{2,1,0:T(4,128)S(1)} %max.4, pred[8,8]{1,0:T(8,128)(4,1)S(1)} %copy.76), kind=kLoop, calls=%fused_computation.8.clone.1 | loop fusion | flops 20967424 | bytes 16810048 | tf_op jit(solution)/shard_map/while/body/reduce_sum | solution.py:45
  278.3 1.0 copy-done.1
  279.3 8.9 %gather_fusion.1 = bf16[64,4,128,64]{3,2,1,0:T(8,128)(2,1)} fusion(bf16[64,4,128,64]{3,2,1,0:T(8,128)(2,1)} %get-tuple-element.241, s32[1024]{0:T(1024)S(1)} %pad_clamp_fusion.2), kind=kCustom, calls=%fused_computation.1.clone.1 | custom fusion | bytes 8388864 | tf_op jit(solution)/shard_map/while/body/gather | solution.py:33
  288.2 10.6 %fusion.44 = f32[8,4,128,64]{2,3,1,0:T(8,128)S(1)} fusion(bf16[8,8,4,128,64]{4,3,2,1,0:T(8,128)(2,1)} %bitcast.84, f32[8,4,8,128,128]{4,3,2,1,0:T(8,128)} %copy-done.1, f32[8,4,128]{2,1,0:T(4,128)S(1)} %max.4, pred[8,8]{1,0:T(8,128)(4,1)S(1)} %copy.76, f32[8,4,128,64]{2,3,1,0:T(8,128)S(1)} %get-tuple-element.221, f32[8,4,128]{2,1,0:T(4,128)S(1)} %bitcast.95), kind=kOutput, calls=%fused_computation.19.clone.1 | convolution fusion | flops 558366720 | bytes 23101504 | tf_op jit(solution)/shard_map/while/body/qhbjk,qjhke->qhbe/dot_general | solution.py:46
  298.8 0.1 fusion.29
  298.9 0.3 copy.50
  299.3 0.3 all_to_all.28
  299.6 0.1 copy.51
  299.7 12.4 %all_to_all.35 = bf16[4,256,256]{1,2,0:T(8,128)(2,1)S(1)} all-to-all(bf16[4,256,256]{1,2,0:T(8,128)(2,1)S(1)} %copy.51), channel_id=1, replica_groups=mesh['pb'=8,'sp'=4] {'sp'}, dimensions={0} | all-to-all | bytes 1048576 | tf_op jit(solution)/shard_map/all_to_all | solution.py:92
  312.1 2.6 fusion.28
  (40 shorter events, 0.2 us)
Async XLA Ops:
  6.5 305.5 %copy-start = (bf16[1024,1024]{1,0:T(8,128)(2,1)S(1)}, bf16[1024,1024]{1,0:T(8,128)(2,1)}, u32[]{:S(2)}) copy-start(bf16[1024,1024]{1,0:T(8,128)(2,1)} %param.9) | copy-start | bytes 6291460
  6.5 89.9 %all-gather.5.cloned.1.call-start = ((), (), s32[]{:S(2)}) async-start(), calls=%async_computation.3 | async-start | bytes 4718592 | tf_op jit(solution)/shard_map/all_gather | solution.py:84
  12.6 36.8 %copy-start.3 = (s32[64]{0:T(128)S(1)}, s32[64]{0:T(128)}, u32[]{:S(2)}) copy-start(s32[64]{0:T(128)} %param.11) | copy-start | bytes 772
  12.6 38.1 %copy-start.2 = (s32[64,32]{0,1:T(8,128)S(1)}, s32[64,32]{0,1:T(8,128)}, u32[]{:S(2)}) copy-start(s32[64,32]{0,1:T(8,128)} %param.10) | copy-start | bytes 24580
  48.6 95.4 %all-gather.3.cloned.1.call-start = ((), (), s32[]{:S(2)}) async-start(), calls=%async_computation.2 | async-start | bytes 4718592 | tf_op jit(solution)/shard_map/all_gather | solution.py:83
  163.0 5.7 %copy-start.1 = (f32[8,4,8,128,128]{4,3,2,1,0:T(8,128)}, f32[8,4,8,128,128]{4,3,2,1,0:T(8,128)S(1)}, u32[]{:S(2)}) copy-start(f32[8,4,8,128,128]{4,3,2,1,0:T(8,128)S(1)} %get-tuple-element.201) | copy-start | bytes 50331652 | tf_op jit(solution)/shard_map/while
  199.8 5.7 %copy-start.1 = (f32[8,4,8,128,128]{4,3,2,1,0:T(8,128)}, f32[8,4,8,128,128]{4,3,2,1,0:T(8,128)S(1)}, u32[]{:S(2)}) copy-start(f32[8,4,8,128,128]{4,3,2,1,0:T(8,128)S(1)} %get-tuple-element.201) | copy-start | bytes 50331652 | tf_op jit(solution)/shard_map/while
  236.7 5.7 %copy-start.1 = (f32[8,4,8,128,128]{4,3,2,1,0:T(8,128)}, f32[8,4,8,128,128]{4,3,2,1,0:T(8,128)S(1)}, u32[]{:S(2)}) copy-start(f32[8,4,8,128,128]{4,3,2,1,0:T(8,128)S(1)} %get-tuple-element.201) | copy-start | bytes 50331652 | tf_op jit(solution)/shard_map/while
  273.6 5.7 %copy-start.1 = (f32[8,4,8,128,128]{4,3,2,1,0:T(8,128)}, f32[8,4,8,128,128]{4,3,2,1,0:T(8,128)S(1)}, u32[]{:S(2)}) copy-start(f32[8,4,8,128,128]{4,3,2,1,0:T(8,128)S(1)} %get-tuple-element.201) | copy-start | bytes 50331652 | tf_op jit(solution)/shard_map/while
Sparse Core Ops, SparseCore 0:
  48.8 47.6 all-gather.4
  98.0 45.9 all-gather.2
where the time goes:
time: 321 us
  local copies, waits for them, and re-layouts  90.2 us (28%)
  waiting for transfers between devices  83.9 us (26%)
  matrix products  75.4 us (23%)
  blocking collectives  37.3 us (12%)
  other arithmetic  20 us (6%)
  between operations  14.1 us (4%)
    all_gather x1, waiting for transfers between devices, shards(): lax.all_gather(value_local, 'pb', axis=0, tiled=True)  44.4 us
    dot_general x4, matrix products, advance(): jnp.einsum('qhbjk,qjhke->qhbe', weights.astype(jnp.bfloat16), fetched_val...  42.2 us
    all_gather x1, waiting for transfers between devices, shards(): lax.all_gather(key_local, 'pb', axis=0, tiled=True)  38.8 us
    gather x4, local copies, waits for them, and re-layouts, advance(): fetched_values = value_table[chosen]  35.5 us
    all_to_all x1, blocking collectives, shards(): lax.all_to_all(projected, 'sp', split_axis=1, concat_axis=0, tiled=True)  24.9 us
    dot_general x4, matrix products, advance(): jnp.einsum('qhbe,qjhek->qhbjk', queries, fetched_keys, preferred_element_...  24.6 us
    gather x4, local copies, waits for them, and re-layouts, advance(): fetched_keys = key_table[chosen]  20.9 us
    reduce_sum x4, other arithmetic, advance(): running_total = running_total * fade_factor + jnp.sum(weights, axis=(3, 4))  18.7 us
  transfers between devices with their start and end apart: 2, of which 2 were waited for; matrix products, arithmetic and copies ran while one was open for 3% of the time, Pallas kernels for 0%

commit v1 on v0

v1 whole, which is shorter than its diff:
```python
import functools

import jax
import jax.numpy as jnp
from jax import lax
from jax.experimental import pallas as pl
from jax.experimental.pallas import tpu as pltpu
from jax.sharding import PartitionSpec as P

HEADS = 16
HEAD_DIM = 64
TILE = 128
PAIR = 2 * HEAD_DIM
PAIRS = HEADS // 2
NEGATIVE = -1e30
TRANSPOSED = (((1,), (1,)), ((), ()))
VMEM_LIMIT = 60 * 1024 * 1024


def query_kernel(x_ref, wq_ref, q_ref):
    q = lax.dot_general(wq_ref[...], x_ref[...], TRANSPOSED, preferred_element_type=jnp.float32)
    q = q.astype(jnp.bfloat16) * jnp.bfloat16(HEAD_DIM ** -0.5)
    for j in range(q_ref.shape[0]):
        q_ref[j] = q[:, j * TILE : (j + 1) * TILE]


def key_value_kernel(x_ref, wk_ref, wv_ref, k_ref, v_ref):
    x = x_ref[...]
    k = lax.dot_general(x, wk_ref[...], TRANSPOSED, preferred_element_type=jnp.float32)
    v = lax.dot_general(wv_ref[...], x, TRANSPOSED, preferred_element_type=jnp.float32)
    k_ref[...] = k.astype(jnp.bfloat16)
    v = v.astype(jnp.bfloat16)
    for j in range(v_ref.shape[0]):
        v_ref[j] = v[:, j * TILE : (j + 1) * TILE]


def project_query(x, wq):
    rows, width = x.shape
    return pl.pallas_call(
        query_kernel,
        out_shape=jax.ShapeDtypeStruct((rows // TILE, width, TILE), jnp.bfloat16),
        compiler_params=pltpu.CompilerParams(vmem_limit_bytes=VMEM_LIMIT),
        cost_estimate=pl.CostEstimate(flops=2 * rows * width * width, bytes_accessed=2 * width * width, transcendentals=0),
        name="query",
    )(x, wq)


def project_key_value(x, wk, wv, step):
    rows, width = x.shape
    return pl.pallas_call(
        key_value_kernel,
        grid=(rows // step,),
        in_specs=[
            pl.BlockSpec((step, width), lambda i: (i, 0)),
            pl.BlockSpec((width, width), lambda i: (0, 0)),
            pl.BlockSpec((width, width), lambda i: (0, 0)),
        ],
        out_specs=[
            pl.BlockSpec((step, width), lambda i: (i, 0)),
            pl.BlockSpec((step // TILE, width, TILE), lambda i: (i, 0, 0)),
        ],
        out_shape=[
            jax.ShapeDtypeStruct((rows, width), jnp.bfloat16),
            jax.ShapeDtypeStruct((rows // TILE, width, TILE), jnp.bfloat16),
        ],
        compiler_params=pltpu.CompilerParams(vmem_limit_bytes=VMEM_LIMIT),
        cost_estimate=pl.CostEstimate(
            flops=4 * rows * width * width, bytes_accessed=6 * rows * width + 4 * width * width, transcendentals=0
        ),
        name="key_value",
    )(x, wk, wv)


def attend_kernel(first, key_tiles, flags, q_ref, k_ref, v_ref, *rest):
    if first:
        acc_ref, m_ref, l_ref, spread = rest
    else:
        acc_in, m_in, l_in, out_ref, stat_ref, spread, acc_ref, m_ref, l_ref = rest
    tile = pl.program_id(0)

    @pl.when(tile == 0)
    def _():
        spread[...] = jnp.zeros_like(spread)

    for p in range(PAIRS):
        low = p * PAIR
        spread[p, :HEAD_DIM, :TILE] = q_ref[0, low : low + HEAD_DIM, :]
        spread[p, HEAD_DIM:, TILE:] = q_ref[0, low + HEAD_DIM : low + PAIR, :]
    if first:
        acc_ref[...] = jnp.zeros_like(acc_ref)
        m_ref[...] = jnp.full_like(m_ref, NEGATIVE)
        l_ref[...] = jnp.zeros_like(l_ref)
    else:
        acc_ref[...] = acc_in[...]
        m_ref[...] = m_in[...]
        l_ref[...] = l_in[...]

    def visit(kt, carry):
        @pl.when(flags[tile * key_tiles + kt] > 0)
        def _():
            rows = pl.ds(pl.multiple_of(kt * TILE, TILE), TILE)
            for p in range(PAIRS):
                low = p * PAIR
                s = jnp.dot(k_ref[rows, low : low + PAIR], spread[p], preferred_element_type=jnp.float32)
                m_old = m_ref[0, p : p + 1, :]
                m_new = jnp.maximum(m_old, jnp.max(s, axis=0, keepdims=True))
                fade = jnp.exp(m_old - m_new)
                w = jnp.exp(s - m_new)
                m_ref[0, p : p + 1, :] = m_new
                l_ref[0, p : p + 1, :] = l_ref[0, p : p + 1, :] * fade + jnp.sum(w, axis=0, keepdims=True)
                w = w.astype(jnp.bfloat16)
                for i in range(2):
                    at = low + i * HEAD_DIM
                    half = slice(i * TILE, (i + 1) * TILE)
                    o = jnp.dot(v_ref[kt, at : at + HEAD_DIM, :], w[:, half], preferred_element_type=jnp.float32)
                    acc_ref[0, at : at + HEAD_DIM, :] = acc_ref[0, at : at + HEAD_DIM, :] * fade[:, half] + o

        return carry

    lax.fori_loop(0, key_tiles, visit, 0)
    if not first:
        total = l_ref[0]
        inverse = jnp.where(total > 0.0, 1.0 / jnp.where(total > 0.0, total, 1.0), 0.0)
        for h in range(HEADS):
            half = slice((h % 2) * TILE, (h % 2 + 1) * TILE)
            at = h * HEAD_DIM
            scaled = acc_ref[0, at : at + HEAD_DIM, :] * inverse[h // 2 : h // 2 + 1, half]
            out_ref[0, at : at + HEAD_DIM, :] = scaled.astype(jnp.bfloat16)
        stat_ref[0, 0] = m_ref[0]
        stat_ref[0, 1] = total


def attend(flags, q, k, v, state=None):
    tiles, width, _ = q.shape
    key_tiles = v.shape[0]
    first = state is None
    per_tile = lambda *shape: pl.BlockSpec((1,) + shape, lambda t, f: (t,) + (0,) * len(shape))
    whole = lambda *shape: pl.BlockSpec(shape, lambda t, f: (0,) * len(shape))
    state_specs = [per_tile(width, TILE), per_tile(PAIRS, 2 * TILE), per_tile(PAIRS, 2 * TILE)]
    state_shapes = [
        jax.ShapeDtypeStruct((tiles, width, TILE), jnp.float32),
        jax.ShapeDtypeStruct((tiles, PAIRS, 2 * TILE), jnp.float32),
        jax.ShapeDtypeStruct((tiles, PAIRS, 2 * TILE), jnp.float32),
    ]
    in_specs = [per_tile(width, TILE), whole(*k.shape), whole(*v.shape)]
    scratch = [pltpu.VMEM((PAIRS, PAIR, 2 * TILE), jnp.bfloat16)]
    if first:
        out_specs, out_shape, extra = state_specs, state_shapes, ()
    else:
        in_specs = in_specs + state_specs
        out_specs = [per_tile(width, TILE), per_tile(2, PAIRS, 2 * TILE)]
        out_shape = [
            jax.ShapeDtypeStruct((tiles, width, TILE), jnp.bfloat16),
            jax.ShapeDtypeStruct((tiles, 2, PAIRS, 2 * TILE), jnp.float32),
        ]
        scratch = scratch + [pltpu.VMEM((1,) + s.shape[1:], s.dtype) for s in state_shapes]
        extra = tuple(state)
    pairs = tiles * 2
    return pl.pallas_call(
        functools.partial(attend_kernel, first, key_tiles),
        grid_spec=pltpu.PrefetchScalarGridSpec(
            num_scalar_prefetch=1, grid=(tiles,), in_specs=in_specs, out_specs=out_specs, scratch_shapes=scratch
        ),
        out_shape=out_shape,
        compiler_params=pltpu.CompilerParams(vmem_limit_bytes=VMEM_LIMIT),
        cost_estimate=pl.CostEstimate(
            flops=8 * pairs * TILE * TILE * width, bytes_accessed=4 * k.size, transcendentals=pairs * HEADS * TILE * TILE
        ),
        name="attend_near" if first else "attend_far",
    )(flags, q, k, v, *extra)


def finish_kernel(count, *refs):
    x_ref, wo_ref = refs[:2]
    parts, stats = refs[2 : 2 + count], refs[2 + count : 2 + 2 * count]
    out_ref, joined = refs[2 + 2 * count :]
    highest = stats[0][0, 0]
    for s in stats[1:]:
        highest = jnp.maximum(highest, s[0, 0])
    shares = [jnp.exp(s[0, 0] - highest) * s[0, 1] for s in stats]
    total = functools.reduce(lambda a, b: a + b, shares)
    shares = [s / total for s in shares]
    for h in range(HEADS):
        half = slice((h % 2) * TILE, (h % 2 + 1) * TILE)
        at = h * HEAD_DIM
        summed = sum(
            part[0, at : at + HEAD_DIM, :].astype(jnp.float32) * share[h // 2 : h // 2 + 1, half]
            for part, share in zip(parts, shares)
        )
        joined[at : at + HEAD_DIM, :] = summed.astype(jnp.bfloat16)
    added = lax.dot_general(
        joined[...], wo_ref[...], (((0,), (0,)), ((), ())), preferred_element_type=jnp.float32
    )
    out_ref[...] = (x_ref[...].astype(jnp.float32) + added).astype(jnp.bfloat16)


def finish(x, wo, parts, stats):
    rows, width = x.shape
    count = len(parts)
    return pl.pallas_call(
        functools.partial(finish_kernel, count),
        grid=(rows // TILE,),
        in_specs=[pl.BlockSpec((TILE, width), lambda i: (i, 0)), pl.BlockSpec((width, width), lambda i: (0, 0))]
        + [pl.BlockSpec((1, width, TILE), lambda i: (i, 0, 0))] * count
        + [pl.BlockSpec((1, 2, PAIRS, 2 * TILE), lambda i: (i, 0, 0, 0))] * count,
        out_specs=pl.BlockSpec((TILE, width), lambda i: (i, 0)),
        out_shape=jax.ShapeDtypeStruct((rows, width), jnp.bfloat16),
        scratch_shapes=[pltpu.VMEM((width, TILE), jnp.bfloat16)],
        compiler_params=pltpu.CompilerParams(vmem_limit_bytes=VMEM_LIMIT),
        name="finish",
    )(x, wo, *parts, *stats)


def shards(nodes, project_in, project_out, tile_list, tile_count):
    rows, width = nodes.shape
    groups, sp = lax.axis_size("pb"), lax.axis_size("sp")
    g, s = lax.axis_index("pb"), lax.axis_index("sp")
    own = rows // TILE
    group_tiles = own * sp
    far = lax.all_gather(nodes, "pb", axis=0, tiled=True)

    def swap(k, value):
        if k == 0:
            return value
        return lax.ppermute(value, "sp", [(i, i ^ k) for i in range(sp)])

    weights = project_in.T.reshape(HEADS, 3, HEAD_DIM, width).transpose(1, 0, 2, 3).reshape(3, width, width)
    wq, wk, wv = weights[0], weights[1], weights[2]
    q_own = project_query(nodes, wq)
    q = jnp.concatenate([swap(k, q_own) for k in range(sp)], axis=0)
    k_own, v_own = project_key_value(nodes, wk, wv, rows)

    partner = s ^ jnp.arange(sp, dtype=jnp.int32)
    local = jnp.arange(own, dtype=jnp.int32)
    q_tiles = (g * group_tiles + partner[:, None] * own + local[None, :]).reshape(-1)
    lists, counts = tile_list[q_tiles], tile_count[q_tiles]
    lists = jnp.where(jnp.arange(lists.shape[1], dtype=jnp.int32)[None, :] < counts[:, None], lists, -1)
    group_ids = jnp.arange(groups, dtype=jnp.int32)
    key_tiles = (group_ids[:, None] * group_tiles + s * own + local[None, :]).reshape(-1)
    used = jnp.any(lists[:, :, None] == key_tiles[None, None, :], axis=1).astype(jnp.int32)
    near = jnp.any(lists[:, :, None] == (g * group_tiles + s * own + local)[None, None, :], axis=1).astype(jnp.int32)
    distant = jnp.where((key_tiles // group_tiles == g)[None, :], 0, used)

    state = attend(near.reshape(-1), q, k_own, v_own)
    k_far, v_far = project_key_value(far, wk, wv, rows)
    part, stat = attend(distant.reshape(-1), q, k_far, v_far, state)
    parts = [swap(k, part[k * own : (k + 1) * own]) for k in range(sp)]
    stats = [swap(k, stat[k * own : (k + 1) * own]) for k in range(sp)]
    return finish(nodes, project_out, parts, stats)


def solution(mesh):
    in_specs = (P(("pb", "sp"), None), P(), P(), P(), P())
    out_specs = P(("pb", "sp"), None)
    return jax.shard_map(shards, mesh=mesh, in_specs=in_specs, out_specs=out_specs, check_vma=False)
```

time: 321 us -> 142 us (0.44)
  matrix products: 75.4 us -> 0 us
  local copies, waits for them, and re-layouts: 90.2 us -> 21.6 us
  Pallas kernels: 0 us -> 52.8 us
  waiting for transfers between devices: 83.9 us -> 35 us
  blocking collectives: 37.3 us -> 0 us
  other arithmetic: 20 us -> 2.37 us
  starting transfers between devices: 0.04 us -> 16.2 us
    all_gather x2 -> x1, waiting for transfers between devices: 83.2 us -> 0.01 us  [shards(): far = lax.all_gather(nodes, 'pb', axis=0, tiled=True)]
    dot_general x10 -> x0, matrix products: 75.4 us -> none  [the longest x4 42.2 us: advance(): jnp.einsum('qhbjk,qjhke->qhbe', weights.astype(jnp.bfloat16), fetched_val...]
    gather x8 -> x2, local copies, waits for them, and re-layouts: 56.4 us -> 1.2 us  [shards(): lists, counts = (tile_list[q_tiles], tile_count[q_tiles])]
    pallas_call x0 -> x6, Pallas kernels: none -> 52.8 us  [the longest x2 26.8 us: attend(): pl.pallas_call(functools.partial(attend_kernel, first, key_tiles), grid_s...]
    all_to_all x2 -> x0, blocking collectives: 37.3 us -> none  [the longest x1 24.9 us: shards(): lax.all_to_all(projected, 'sp', split_axis=1, concat_axis=0, tiled=True)]
    ppermute x0 -> x9, waiting for transfers between devices: none -> 34.3 us  [swap(): return lax.ppermute(value, 'sp', [(i, i ^ k) for i in range(sp)])]
    while x15 -> x0, local copies, waits for them, and re-layouts: 20.8 us -> none  [the longest x3 16.7 us: attend(): lax.fori_loop(0, blocks, advance, start_state)]
    reduce_sum x4 -> x0, other arithmetic: 18.7 us -> none  [advance(): running_total = running_total * fade_factor + jnp.sum(weights, axis=(3, 4))]
  transfers between devices with their start and end apart: 2 -> 10, of which waited for: 2 -> 5; matrix products, arithmetic and copies ran while one was open for 3% -> 14% of each run, Pallas kernels for 0% -> 13%
where the time goes in v1:
time: 142 us
  Pallas kernels  52.8 us (37%)
  waiting for transfers between devices  35 us (25%)
  local copies, waits for them, and re-layouts  21.6 us (15%)
  starting transfers between devices  16.2 us (11%)
  between operations  13.5 us (10%)
  other arithmetic  2.37 us (2%)
    ppermute x9, waiting for transfers between devices, swap(): return lax.ppermute(value, 'sp', [(i, i ^ k) for i in range(sp)])  34.3 us
    pallas_call x2, Pallas kernels, attend(): pl.pallas_call(functools.partial(attend_kernel, first, key_tiles), grid_s...  26.8 us
    pallas_call x2, Pallas kernels, project_key_value(): pl.pallas_call(key_value_kernel, grid=(rows // step,), in_specs=[pl.Block...  18.2 us
    ppermute x9, starting transfers between devices, swap(): return lax.ppermute(value, 'sp', [(i, i ^ k) for i in range(sp)])  16.2 us
    unnamed x22, local copies, waits for them, and re-layouts  9.86 us
    slice x1, local copies, waits for them, and re-layouts, shards(): wq, wk, wv = (weights[0], weights[1], weights[2])  5.96 us
    pallas_call x1, Pallas kernels, finish(): pl.pallas_call(functools.partial(finish_kernel, count), grid=(rows // TIL...  4.52 us
    pallas_call x1, Pallas kernels, project_query(): pl.pallas_call(query_kernel, out_shape=jax.ShapeDtypeStruct((rows // TILE...  3.32 us
  transfers between devices with their start and end apart: 10, of which 5 were waited for; matrix products, arithmetic and copies ran while one was open for 14% of the time, Pallas kernels for 13%

profile of v1, /device:TPU:0, one launch (start us, length us, event | category | flops | bytes accessed | tf_op | source)
XLA Modules:
  0.0 141.6 jit_solution(3458271936326564617)
XLA Ops:
  6.5 0.0 copy-start
  6.5 0.0 all-gather.2.cloned.1.call-start
  6.5 0.7 all-gather.2.cloned.1.call-update
  7.3 8.6 %copy.11 = bf16[1024,3072]{0,1:T(8,128)(2,1)} copy(bf16[1024,3072]{1,0:T(8,128)(2,1)} %param.6) | data formatting | bytes 12582912 | tf_op args[1]
  15.9 6.0 %fusion.3 = (bf16[1,16,64,1024]{3,2,0,1:T(8,128)(2,1)}, bf16[1,16,64,1024]{3,2,0,1:T(8,128)(2,1)}, bf16[1,16,64,1024]{3,2,0,1:T(8,128)(2,1)}) fusion(bf16[3,16,64,1024]{3,2,0,1:T(8,128)(2,1)} %bitcast.10), kind=kLoop, calls=%fused_computation.21 | loop fusion | bytes 12582912 | tf_op jit(solution)/shard_map/slice | solution.py:228
  21.9 0.0 copy-start.9
  21.9 3.3 %query.1 = bf16[2,1024,128]{2,1,0:T(8,128)(2,1)} custom-call(bf16[256,1024]{1,0:T(8,128)(2,1)} %refs_0_.1, bf16[1024,1024]{1,0:T(8,128)(2,1)} %bitcast.15), custom_call_target="tpu_custom_call" | custom-call | flops 536870912 | bytes 2097152 | tf_op jit(solution)/shard_map/query/pallas_call | solution.py:39
  25.2 4.1 %collective-permute-start.2 = (bf16[2,1024,128]{2,1,0:T(8,128)(2,1)}, bf16[2,1024,128]{2,1,0:T(8,128)(2,1)S(1)}, u32[]{:S(2)}, u32[]{:S(2)}) collective-permute-start(bf16[2,1024,128]{2,1,0:T(8,128)(2,1)} %query.1), channel_id=1, source_target_pairs={{0,3},{1,2},{2,1},{3,0},{4,7},{5,6},{6,5},{7,4},{8,11},{9,10},{10,... | collective-permute-start | bytes 1572872 | tf_op jit(solution)/shard_map/ppermute | solution.py:225
  29.2 0.5 collective-permute-start.1
  29.7 0.1 collective-permute-start
  29.8 0.0 copy-done.9
  29.8 0.1 copy.10
  29.9 0.1 iota_add_fusion.1
  30.0 0.1 add.111
  30.1 0.6 gather_fusion.1
  30.6 0.0 copy-done
  30.6 0.6 gather_fusion
  31.3 0.1 iota_add_fusion
  31.4 0.1 add.105
  31.5 0.1 fusion
  31.5 0.3 compare_reduce_fusion
  31.9 0.6 select_n.40.flags
  32.5 0.2 compare_reduce_fusion.1
  32.7 0.1 copy.12
  32.8 0.7 reshape.136.flags
  33.4 0.0 copy-start.1
  33.4 4.5 %key_value.3 = (bf16[256,1024]{1,0:T(8,128)(2,1)}, bf16[2,1024,128]{2,1,0:T(8,128)(2,1)}) custom-call(bf16[256,1024]{1,0:T(8,128)(2,1)} %refs_0_.1, bf16[1024,1024]{1,0:T(8,128)(2,1)} %bitcast.13, bf16[1024,1024]{1,0:T(8,128)(2,1)} %bitcast.11), custom_call_target="tpu_custom_call" | custom-call | flops 1073741824 | bytes 5767168 | tf_op jit(solution)/shard_map/key_value/pallas_call | solution.py:50
  38.0 4.3 %collective-permute-done.2 = bf16[2,1024,128]{2,1,0:T(8,128)(2,1)S(1)} collective-permute-done((bf16[2,1024,128]{2,1,0:T(8,128)(2,1)}, bf16[2,1024,128]{2,1,0:T(8,128)(2,1)S(1)}, u32[]{:S(2)}, u32[]{:S(2)}) %collective-permute-start.2) | collective-permute-done | bytes 524320 | tf_op jit(solution)/shard_map/ppermute | solution.py:225
  42.3 10.3 %collective-permute-done.1 = bf16[2,1024,128]{2,1,0:T(8,128)(2,1)S(1)} collective-permute-done((bf16[2,1024,128]{2,1,0:T(8,128)(2,1)}, bf16[2,1024,128]{2,1,0:T(8,128)(2,1)S(1)}, u32[]{:S(2)}, u32[]{:S(2)}) %collective-permute-start.1) | collective-permute-done | bytes 524320 | tf_op jit(solution)/shard_map/ppermute | solution.py:225
  52.6 0.3 collective-permute-done
  52.9 0.0 copy-done.1
  52.9 1.6 %pad_maximum_fusion.q_ref = bf16[8,1024,128]{2,1,0:T(8,128)(2,1)} fusion(bf16[2,1024,128]{2,1,0:T(8,128)(2,1)S(1)} %collective-permute-done.2, bf16[2,1024,128]{2,1,0:T(8,128)(2,1)S(1)} %collective-permute-done.1, bf16[2,1024,128]{2,1,0:T(8,128)(2,1)S(1)} %collective-permute-done, bf16[2,1024,128]{2,1,0:T(8,128)(2,1)S(1)} %copy-done.1), kind=kLoop, calls=%fused_computation.2 | loop fusion | flops 3145728 | bytes 4194304 | tf_op jit(solution)/shard_map/concatenate | solution.py:230
  54.5 11.2 %attend_near.1 = (f32[8,1024,128]{2,1,0:T(8,128)}, f32[8,8,256]{2,1,0:T(8,128)}, f32[8,8,256]{2,1,0:T(8,128)}) custom-call(s32[16]{0:T(128)} %reshape.136.flags, bf16[8,1024,128]{2,1,0:T(8,128)(2,1)} %pad_maximum_fusion.q_ref, bf16[256,1024]{1,0:T(8,128)(2,1)} %get-tuple-element.16.k_ref, bf16[2,1024,128]{2,1,0:T(8,128)(2,1)} %get-tuple-element.17.v_ref), custom_call_target="tpu_custom_call" | custom-call | flops 2147483648 | bytes 1048576 | tf_op jit(solution)/shard_map/attend_near/pallas_call | solution.py:159
  65.7 0.0 all-gather.2.cloned.1.call-done.x_ref
  65.7 13.7 %key_value.2 = (bf16[2048,1024]{1,0:T(8,128)(2,1)}, bf16[16,1024,128]{2,1,0:T(8,128)(2,1)}) custom-call(bf16[2048,1024]{1,0:T(8,128)(2,1)} %all-gather.2.cloned.1.call-done.x_ref, bf16[1024,1024]{1,0:T(8,128)(2,1)} %bitcast.14, bf16[1024,1024]{1,0:T(8,128)(2,1)} %bitcast.12), custom_call_target="tpu_custom_call" | custom-call | flops 8589934592 | bytes 16777216 | tf_op jit(solution)/shard_map/key_value/pallas_call | solution.py:50
  79.4 15.6 %attend_far.1 = (bf16[8,1024,128]{2,1,0:T(8,128)(2,1)}, f32[8,2,8,256]{3,2,1,0:T(8,128)}) custom-call(s32[128]{0:T(128)} %select_n.40.flags, bf16[8,1024,128]{2,1,0:T(8,128)(2,1)} %pad_maximum_fusion.q_ref, bf16[2048,1024]{1,0:T(8,128)(2,1)} %get-tuple-element.14.k_ref, bf16[16,1024,128]{2,1,0:T(8,128)(2,1)} %get-tuple-element.15.v_ref, ...), custom_call_target="tpu_custom_call" | custom-call | flops 2147483648 | bytes 8388608 | tf_op jit(solution)/shard_map/attend_far/pallas_call | solution.py:159
  95.0 0.0 copy-start.5
  95.0 2.5 %fusion.4 = (bf16[2,1024,128]{2,1,0:T(8,128)(2,1)S(1)}, bf16[2,1024,128]{2,1,0:T(8,128)(2,1)S(1)}, bf16[2,1024,128]{2,1,0:T(8,128)(2,1)S(1)}, bf16[2,1024,128]{2,1,0:T(8,128)(2,1)}) fusion(bf16[8,1024,128]{2,1,0:T(8,128)(2,1)} %get-tuple-element.21), kind=kLoop, calls=%fused_computation.22 | loop fusion | bytes 4194304 | tf_op jit(solution)/shard_map/slice | solution.py:247
  97.5 0.0 collective-permute-start.3
  97.5 5.2 %collective-permute-start.4 = (bf16[2,1024,128]{2,1,0:T(8,128)(2,1)S(1)}, bf16[2,1024,128]{2,1,0:T(8,128)(2,1)S(1)}, u32[]{:S(2)}, u32[]{:S(2)}) collective-permute-start(bf16[2,1024,128]{2,1,0:T(8,128)(2,1)S(1)} %get-tuple-element.27), channel_id=1, source_target_pairs={{0,2},{1,3},{2,0},{3,1},{4,6},{5,7},{6,4},{7,5},{8,10},{9,11},{10,... | collective-permute-start | bytes 1572872 | tf_op jit(solution)/shard_map/ppermute | solution.py:225
  102.7 0.0 collective-permute-start.5
  102.7 0.0 copy-done.5
  102.7 0.6 fusion.5
  103.3 1.5 %collective-permute-start.6 = (f32[2,2,8,256]{3,2,1,0:T(8,128)S(1)}, f32[2,2,8,256]{3,2,1,0:T(8,128)S(1)}, u32[]{:S(2)}, u32[]{:S(2)}) collective-permute-start(f32[2,2,8,256]{3,2,1,0:T(8,128)S(1)} %get-tuple-element.32), channel_id=1, source_target_pairs={{0,1},{1,0},{2,3},{3,2},{4,5},{5,4},{6,7},{7,6},{8,9},{9,8},{10,11... | collective-permute-start | bytes 98312 | tf_op jit(solution)/shard_map/ppermute | solution.py:225
  104.8 2.0 %collective-permute-start.7 = (f32[2,2,8,256]{3,2,1,0:T(8,128)S(1)}, f32[2,2,8,256]{3,2,1,0:T(8,128)S(1)}, u32[]{:S(2)}, u32[]{:S(2)}) collective-permute-start(f32[2,2,8,256]{3,2,1,0:T(8,128)S(1)} %get-tuple-element.31), channel_id=1, source_target_pairs={{0,2},{1,3},{2,0},{3,1},{4,6},{5,7},{6,4},{7,5},{8,10},{9,11},{10,... | collective-permute-start | bytes 98312 | tf_op jit(solution)/shard_map/ppermute | solution.py:225
  106.8 17.5 %collective-permute-done.6.refs_7_ = f32[2,2,8,256]{3,2,1,0:T(8,128)S(1)} collective-permute-done((f32[2,2,8,256]{3,2,1,0:T(8,128)S(1)}, f32[2,2,8,256]{3,2,1,0:T(8,128)S(1)}, u32[]{:S(2)}, u32[]{:S(2)}) %collective-permute-start.6) | collective-permute-done | bytes 32800 | tf_op jit(solution)/shard_map/ppermute | solution.py:225
  124.2 0.0 copy-start.6
  124.2 2.9 %collective-permute-start.8 = (f32[2,2,8,256]{3,2,1,0:T(8,128)S(1)}, f32[2,2,8,256]{3,2,1,0:T(8,128)S(1)}, u32[]{:S(2)}, u32[]{:S(2)}) collective-permute-start(f32[2,2,8,256]{3,2,1,0:T(8,128)S(1)} %get-tuple-element.30), channel_id=1, source_target_pairs={{0,3},{1,2},{2,1},{3,0},{4,7},{5,6},{6,5},{7,4},{8,11},{9,10},{10,... | collective-permute-start | bytes 98312 | tf_op jit(solution)/shard_map/ppermute | solution.py:225
  127.1 0.0 collective-permute-done.7.refs_8_
  127.1 0.0 copy-start.7
  127.1 1.9 %collective-permute-done.8.refs_9_ = f32[2,2,8,256]{3,2,1,0:T(8,128)S(1)} collective-permute-done((f32[2,2,8,256]{3,2,1,0:T(8,128)S(1)}, f32[2,2,8,256]{3,2,1,0:T(8,128)S(1)}, u32[]{:S(2)}, u32[]{:S(2)}) %collective-permute-start.8) | collective-permute-done | bytes 32800 | tf_op jit(solution)/shard_map/ppermute | solution.py:225
  129.0 0.0 copy-start.8
  129.0 0.0 collective-permute-done.3.refs_3_
  129.1 0.0 collective-permute-done.4.refs_4_
  129.1 0.0 copy-start.3
  129.1 0.0 collective-permute-done.5.refs_5_
  129.1 0.0 copy-start.4
  129.1 0.0 copy-done.6
  129.1 0.0 copy-done.7
  129.1 0.5 copy-done.8
  129.7 0.2 copy-done.2
  129.9 0.2 copy-done.3
  130.1 0.2 copy-done.4
  130.2 4.5 %finish.1 = bf16[256,1024]{1,0:T(8,128)(2,1)} custom-call(bf16[256,1024]{1,0:T(8,128)(2,1)} %refs_0_.1, bf16[1024,1024]{1,0:T(8,128)(2,1)} %refs_1_.1, bf16[2,1024,128]{2,1,0:T(8,128)(2,1)} %get-tuple-element.29.refs_2_, bf16[2,1024,128]{2,1,0:T(8,128)(2,1)} %copy-done.2, bf16[2,1024,128]{2,1,0:T(8,128)(2,1)} %copy-done.3, bf16[2,1024,128]{2,1,0:T(8,128)(2,1)} %copy-done.4, ...), custom_call_target="tpu_custom_call" | custom-call | tf_op jit(solution)/shard_map/finish/pallas_call | solution.py:200
  (9 shorter events, 0.1 us)
Async XLA Ops:
  6.5 24.1 %copy-start = (s32[64]{0:T(128)S(1)}, s32[64]{0:T(128)}, u32[]{:S(2)}) copy-start(s32[64]{0:T(128)} %param.9) | copy-start | bytes 772
  6.5 59.1 %all-gather.2.cloned.1.call-start = ((), (), s32[]{:S(2)}) async-start(), calls=%async_computation | async-start | bytes 4718592 | tf_op jit(solution)/shard_map/all_gather | solution.py:220
  21.9 8.0 %copy-start.9 = (s32[64,32]{0,1:T(8,128)S(1)}, s32[64,32]{0,1:T(8,128)}, u32[]{:S(2)}) copy-start(s32[64,32]{0,1:T(8,128)} %param.8) | copy-start | bytes 24580
  25.2 17.1 %collective-permute-start.2 = (bf16[2,1024,128]{2,1,0:T(8,128)(2,1)}, bf16[2,1024,128]{2,1,0:T(8,128)(2,1)S(1)}, u32[]{:S(2)}, u32[]{:S(2)}) collective-permute-start(bf16[2,1024,128]{2,1,0:T(8,128)(2,1)} %query.1), channel_id=1, source_target_pairs={{0,3},{1,2},{2,1},{3,0},{4,7},{5,6},{6,5},{7,4},{8,11},{9,10},{10,... | collective-permute-start | bytes 1572872 | tf_op jit(solution)/shard_map/ppermute | solution.py:225
  29.2 23.4 %collective-permute-start.1 = (bf16[2,1024,128]{2,1,0:T(8,128)(2,1)}, bf16[2,1024,128]{2,1,0:T(8,128)(2,1)S(1)}, u32[]{:S(2)}, u32[]{:S(2)}) collective-permute-start(bf16[2,1024,128]{2,1,0:T(8,128)(2,1)} %query.1), channel_id=1, source_target_pairs={{0,2},{1,3},{2,0},{3,1},{4,6},{5,7},{6,4},{7,5},{8,10},{9,11},{10,... | collective-permute-start | bytes 1572872 | tf_op jit(solution)/shard_map/ppermute | solution.py:225
  29.7 23.1 %collective-permute-start = (bf16[2,1024,128]{2,1,0:T(8,128)(2,1)}, bf16[2,1024,128]{2,1,0:T(8,128)(2,1)S(1)}, u32[]{:S(2)}, u32[]{:S(2)}) collective-permute-start(bf16[2,1024,128]{2,1,0:T(8,128)(2,1)} %query.1), channel_id=1, source_target_pairs={{0,1},{1,0},{2,3},{3,2},{4,5},{5,4},{6,7},{7,6},{8,9},{9,8},{10,11... | collective-permute-start | bytes 1572872 | tf_op jit(solution)/shard_map/ppermute | solution.py:225
  33.4 19.5 %copy-start.1 = (bf16[2,1024,128]{2,1,0:T(8,128)(2,1)S(1)}, bf16[2,1024,128]{2,1,0:T(8,128)(2,1)}, u32[]{:S(2)}) copy-start(bf16[2,1024,128]{2,1,0:T(8,128)(2,1)} %query.1) | copy-start | bytes 1572868
  95.0 7.7 %copy-start.5 = (f32[8,2,8,256]{3,2,1,0:T(8,128)S(1)}, f32[8,2,8,256]{3,2,1,0:T(8,128)}, u32[]{:S(2)}) copy-start(f32[8,2,8,256]{3,2,1,0:T(8,128)} %get-tuple-element.22) | copy-start | bytes 393220
  97.5 31.6 %collective-permute-start.3 = (bf16[2,1024,128]{2,1,0:T(8,128)(2,1)S(1)}, bf16[2,1024,128]{2,1,0:T(8,128)(2,1)S(1)}, u32[]{:S(2)}, u32[]{:S(2)}) collective-permute-start(bf16[2,1024,128]{2,1,0:T(8,128)(2,1)S(1)} %get-tuple-element.28), channel_id=1, source_target_pairs={{0,1},{1,0},{2,3},{3,2},{4,5},{5,4},{6,7},{7,6},{8,9},{9,8},{10,11... | collective-permute-start | bytes 1572872 | tf_op jit(solution)/shard_map/ppermute | solution.py:225
  97.5 31.6 %collective-permute-start.4 = (bf16[2,1024,128]{2,1,0:T(8,128)(2,1)S(1)}, bf16[2,1024,128]{2,1,0:T(8,128)(2,1)S(1)}, u32[]{:S(2)}, u32[]{:S(2)}) collective-permute-start(bf16[2,1024,128]{2,1,0:T(8,128)(2,1)S(1)} %get-tuple-element.27), channel_id=1, source_target_pairs={{0,2},{1,3},{2,0},{3,1},{4,6},{5,7},{6,4},{7,5},{8,10},{9,11},{10,... | collective-permute-start | bytes 1572872 | tf_op jit(solution)/shard_map/ppermute | solution.py:225
  102.7 26.4 %collective-permute-start.5 = (bf16[2,1024,128]{2,1,0:T(8,128)(2,1)S(1)}, bf16[2,1024,128]{2,1,0:T(8,128)(2,1)S(1)}, u32[]{:S(2)}, u32[]{:S(2)}) collective-permute-start(bf16[2,1024,128]{2,1,0:T(8,128)(2,1)S(1)} %get-tuple-element.26), channel_id=1, source_target_pairs={{0,3},{1,2},{2,1},{3,0},{4,7},{5,6},{6,5},{7,4},{8,11},{9,10},{10,... | collective-permute-start | bytes 1572872 | tf_op jit(solution)/shard_map/ppermute | solution.py:225
  103.3 20.9 %collective-permute-start.6 = (f32[2,2,8,256]{3,2,1,0:T(8,128)S(1)}, f32[2,2,8,256]{3,2,1,0:T(8,128)S(1)}, u32[]{:S(2)}, u32[]{:S(2)}) collective-permute-start(f32[2,2,8,256]{3,2,1,0:T(8,128)S(1)} %get-tuple-element.32), channel_id=1, source_target_pairs={{0,1},{1,0},{2,3},{3,2},{4,5},{5,4},{6,7},{7,6},{8,9},{9,8},{10,11... | collective-permute-start | bytes 98312 | tf_op jit(solution)/shard_map/ppermute | solution.py:225
  104.8 22.4 %collective-permute-start.7 = (f32[2,2,8,256]{3,2,1,0:T(8,128)S(1)}, f32[2,2,8,256]{3,2,1,0:T(8,128)S(1)}, u32[]{:S(2)}, u32[]{:S(2)}) collective-permute-start(f32[2,2,8,256]{3,2,1,0:T(8,128)S(1)} %get-tuple-element.31), channel_id=1, source_target_pairs={{0,2},{1,3},{2,0},{3,1},{4,6},{5,7},{6,4},{7,5},{8,10},{9,11},{10,... | collective-permute-start | bytes 98312 | tf_op jit(solution)/shard_map/ppermute | solution.py:225
  124.2 4.9 %copy-start.6 = (f32[2,2,8,256]{3,2,1,0:T(8,128)}, f32[2,2,8,256]{3,2,1,0:T(8,128)S(1)}, u32[]{:S(2)}) copy-start(f32[2,2,8,256]{3,2,1,0:T(8,128)S(1)} %collective-permute-done.6.refs_7_) | copy-start | bytes 98308
  124.2 4.8 %collective-permute-start.8 = (f32[2,2,8,256]{3,2,1,0:T(8,128)S(1)}, f32[2,2,8,256]{3,2,1,0:T(8,128)S(1)}, u32[]{:S(2)}, u32[]{:S(2)}) collective-permute-start(f32[2,2,8,256]{3,2,1,0:T(8,128)S(1)} %get-tuple-element.30), channel_id=1, source_target_pairs={{0,3},{1,2},{2,1},{3,0},{4,7},{5,6},{6,5},{7,4},{8,11},{9,10},{10,... | collective-permute-start | bytes 98312 | tf_op jit(solution)/shard_map/ppermute | solution.py:225
  127.1 2.0 %copy-start.7 = (f32[2,2,8,256]{3,2,1,0:T(8,128)}, f32[2,2,8,256]{3,2,1,0:T(8,128)S(1)}, u32[]{:S(2)}) copy-start(f32[2,2,8,256]{3,2,1,0:T(8,128)S(1)} %collective-permute-done.7.refs_8_) | copy-start | bytes 98308
  129.0 0.6 copy-start.8
  129.1 0.8 copy-start.2
  129.1 1.0 copy-start.3
  129.1 1.1 copy-start.4
Sparse Core Ops, SparseCore 0:
  8.9 49.5 all-gather.1

commit v2 on v1

--- a/solution.py
+++ b/solution.py
@@ -14,14 +14,22 @@
 PAIRS = HEADS // 2
 NEGATIVE = -1e30
 TRANSPOSED = (((1,), (1,)), ((), ()))
-VMEM_LIMIT = 60 * 1024 * 1024
-
-
-def query_kernel(x_ref, wq_ref, q_ref):
-    q = lax.dot_general(wq_ref[...], x_ref[...], TRANSPOSED, preferred_element_type=jnp.float32)
-    q = q.astype(jnp.bfloat16) * jnp.bfloat16(HEAD_DIM ** -0.5)
+MIB = 1024 * 1024
+VMEM_LIMIT = 20 * MIB
+
+
+def own_kernel(x_ref, w_ref, q_ref, k_ref, v_ref):
+    y = jnp.dot(x_ref[...], w_ref[...], preferred_element_type=jnp.float32)
+    turned = y.T
+    e = HEAD_DIM
+    q = jnp.concatenate([turned[:e], turned[3 * e : 4 * e]], axis=0).astype(jnp.bfloat16)
+    q = q * jnp.bfloat16(HEAD_DIM ** -0.5)
+    k = jnp.concatenate([turned[e : 2 * e], turned[4 * e : 5 * e]], axis=0)
+    v = jnp.concatenate([turned[2 * e : 3 * e], turned[5 * e :]], axis=0).astype(jnp.bfloat16)
+    k_ref[...] = k.T.astype(jnp.bfloat16)
     for j in range(q_ref.shape[0]):
         q_ref[j] = q[:, j * TILE : (j + 1) * TILE]
+        v_ref[j] = v[:, j * TILE : (j + 1) * TILE]
 
 
 def key_value_kernel(x_ref, wk_ref, wv_ref, k_ref, v_ref):
@@ -34,15 +42,23 @@
         v_ref[j] = v[:, j * TILE : (j + 1) * TILE]
 
 
-def project_query(x, wq):
+def project_own(x, w):
     rows, width = x.shape
-    return pl.pallas_call(
-        query_kernel,
-        out_shape=jax.ShapeDtypeStruct((rows // TILE, width, TILE), jnp.bfloat16),
-        compiler_params=pltpu.CompilerParams(vmem_limit_bytes=VMEM_LIMIT),
-        cost_estimate=pl.CostEstimate(flops=2 * rows * width * width, bytes_accessed=2 * width * width, transcendentals=0),
-        name="query",
-    )(x, wq)
+    turned = jax.ShapeDtypeStruct((rows // TILE, width, TILE), jnp.bfloat16)
+    turned_spec = pl.BlockSpec((rows // TILE, PAIR, TILE), lambda p: (0, p, 0))
+    return pl.pallas_call(
+        own_kernel,
+        grid=(PAIRS,),
+        in_specs=[
+            pl.BlockSpec((rows, width), lambda p: (0, 0)),
+            pl.BlockSpec((width, 3 * PAIR), lambda p: (0, p)),
+        ],
+        out_specs=[turned_spec, pl.BlockSpec((rows, PAIR), lambda p: (0, p)), turned_spec],
+        out_shape=[turned, jax.ShapeDtypeStruct((rows, width), jnp.bfloat16), turned],
+        compiler_params=pltpu.CompilerParams(vmem_limit_bytes=16 * 1024 * 1024),
+        cost_estimate=pl.CostEstimate(flops=6 * rows * width * width, bytes_accessed=6 * width * width, transcendentals=0),
+        name="own",
+    )(x, w)
 
 
 def project_key_value(x, wk, wv, step):
@@ -71,7 +87,7 @@
     )(x, wk, wv)
 
 
-def attend_kernel(first, key_tiles, flags, q_ref, k_ref, v_ref, *rest):
+def attend_kernel(first, offset, key_tiles, flags, q_ref, k_ref, v_ref, *rest):
     if first:
         acc_ref, m_ref, l_ref, spread = rest
     else:
@@ -96,7 +112,7 @@
         l_ref[...] = l_in[...]
 
     def visit(kt, carry):
-        @pl.when(flags[tile * key_tiles + kt] > 0)
+        @pl.when(flags[(tile + offset) * key_tiles + kt] > 0)
         def _():
             rows = pl.ds(pl.multiple_of(kt * TILE, TILE), TILE)
             for p in range(PAIRS):
@@ -130,7 +146,7 @@
         stat_ref[0, 1] = total
 
 
-def attend(flags, q, k, v, state=None):
+def attend(flags, offset, q, k, v, state=None):
     tiles, width, _ = q.shape
     key_tiles = v.shape[0]
     first = state is None
@@ -157,12 +173,12 @@
         extra = tuple(state)
     pairs = tiles * 2
     return pl.pallas_call(
-        functools.partial(attend_kernel, first, key_tiles),
+        functools.partial(attend_kernel, first, offset, key_tiles),
         grid_spec=pltpu.PrefetchScalarGridSpec(
             num_scalar_prefetch=1, grid=(tiles,), in_specs=in_specs, out_specs=out_specs, scratch_shapes=scratch
         ),
         out_shape=out_shape,
-        compiler_params=pltpu.CompilerParams(vmem_limit_bytes=VMEM_LIMIT),
+        compiler_params=pltpu.CompilerParams(vmem_limit_bytes=4 * (k.size + v.size) + 8 * MIB),
         cost_estimate=pl.CostEstimate(
             flops=8 * pairs * TILE * TILE * width, bytes_accessed=4 * k.size, transcendentals=pairs * HEADS * TILE * TILE
         ),
@@ -224,11 +240,10 @@
             return value
         return lax.ppermute(value, "sp", [(i, i ^ k) for i in range(sp)])
 
-    weights = project_in.T.reshape(HEADS, 3, HEAD_DIM, width).transpose(1, 0, 2, 3).reshape(3, width, width)
-    wq, wk, wv = weights[0], weights[1], weights[2]
-    q_own = project_query(nodes, wq)
-    q = jnp.concatenate([swap(k, q_own) for k in range(sp)], axis=0)
-    k_own, v_own = project_key_value(nodes, wk, wv, rows)
+    q_own, k_own, v_own = project_own(nodes, project_in)
+    queries = [swap(k, q_own) for k in range(sp)]
+    weights = project_in.T.reshape(HEADS, 3, HEAD_DIM, width)
+    wk, wv = weights[:, 1].reshape(width, width), weights[:, 2].reshape(width, width)
 
     partner = s ^ jnp.arange(sp, dtype=jnp.int32)
     local = jnp.arange(own, dtype=jnp.int32)
@@ -241,11 +256,13 @@
     near = jnp.any(lists[:, :, None] == (g * group_tiles + s * own + local)[None, None, :], axis=1).astype(jnp.int32)
     distant = jnp.where((key_tiles // group_tiles == g)[None, :], 0, used)
 
-    state = attend(near.reshape(-1), q, k_own, v_own)
+    near, distant = near.reshape(-1), distant.reshape(-1)
+    states = [attend(near, k * own, queries[k], k_own, v_own) for k in range(sp)]
     k_far, v_far = project_key_value(far, wk, wv, rows)
-    part, stat = attend(distant.reshape(-1), q, k_far, v_far, state)
-    parts = [swap(k, part[k * own : (k + 1) * own]) for k in range(sp)]
-    stats = [swap(k, stat[k * own : (k + 1) * own]) for k in range(sp)]
+    parts, stats = [None] * sp, [None] * sp
+    for k in reversed(range(sp)):
+        part, stat = attend(distant, k * own, queries[k], k_far, v_far, states[k])
+        parts[k], stats[k] = swap(k, part), swap(k, stat)
     return finish(nodes, project_out, parts, stats)
 
 

time: 142 us -> 118 us (0.83)
  Pallas kernels: 52.8 us -> 38.4 us
  waiting for transfers between devices: 35 us -> 21 us
  local copies, waits for them, and re-layouts: 21.6 us -> 27.7 us
  other arithmetic: 2.37 us -> 0.76 us
  starting transfers between devices: 16.2 us -> 14.7 us
    ppermute x9, waiting for transfers between devices: 34.3 us -> 15.7 us  [swap(): return lax.ppermute(value, 'sp', [(i, i ^ k) for i in range(sp)])]
    unnamed x22 -> x48, local copies, waits for them, and re-layouts: 9.86 us -> 21.8 us
    pallas_call x2 -> x1, Pallas kernels: 18.2 us -> 10.4 us  [project_key_value(): pl.pallas_call(key_value_kernel, grid=(rows // step,), in_specs=[pl.Block...]
    slice x3 -> x1, local copies, waits for them, and re-layouts: 9.06 us -> 4.37 us  [shards(): weights[:, 2].reshape(width, width)]
    all_gather x1, waiting for transfers between devices: 0.01 us -> 4.58 us  [shards(): far = lax.all_gather(nodes, 'pb', axis=0, tiled=True)]
    pallas_call x3 -> x9, Pallas kernels: 30.1 us -> 25.8 us  [the longest x8 19.9 us: attend(): pl.pallas_call(functools.partial(attend_kernel, first, offset, key_tiles)...]
    pallas_call x1, Pallas kernels: 4.52 us -> 2.19 us  [finish(): pl.pallas_call(functools.partial(finish_kernel, count), grid=(rows // TIL...]
    concatenate x1 -> x0, other arithmetic: 1.6 us -> none  [shards(): q = jnp.concatenate([swap(k, q_own) for k in range(sp)], axis=0)]
  transfers between devices with their start and end apart: 10 -> 10, of which waited for: 5 -> 4; matrix products, arithmetic and copies ran while one was open for 14% -> 13% of each run, Pallas kernels for 13% -> 20%
where the time goes in v2:
time: 118 us; the launch traced here: 116 us
  Pallas kernels  38.4 us (33%)
  local copies, waits for them, and re-layouts  27.7 us (23%)
  waiting for transfers between devices  21 us (18%)
  starting transfers between devices  14.7 us (12%)
  between operations  13.6 us (12%)
    unnamed x48, local copies, waits for them, and re-layouts  21.8 us
    pallas_call x8, Pallas kernels, attend(): pl.pallas_call(functools.partial(attend_kernel, first, offset, key_tiles)...  19.9 us
    ppermute x9, waiting for transfers between devices, swap(): return lax.ppermute(value, 'sp', [(i, i ^ k) for i in range(sp)])  15.7 us
    ppermute x9, starting transfers between devices, swap(): return lax.ppermute(value, 'sp', [(i, i ^ k) for i in range(sp)])  14.7 us
    pallas_call x1, Pallas kernels, project_key_value(): pl.pallas_call(key_value_kernel, grid=(rows // step,), in_specs=[pl.Block...  10.4 us
    pallas_call x1, Pallas kernels, project_own(): pl.pallas_call(own_kernel, grid=(PAIRS,), in_specs=[pl.BlockSpec((rows, w...  5.9 us
    all_gather x1, waiting for transfers between devices, shards(): far = lax.all_gather(nodes, 'pb', axis=0, tiled=True)  4.58 us
    slice x1, local copies, waits for them, and re-layouts, shards(): weights[:, 2].reshape(width, width)  4.37 us
  transfers between devices with their start and end apart: 10, of which 4 were waited for; matrix products, arithmetic and copies ran while one was open for 13% of the time, Pallas kernels for 20%

profile of v2, /device:TPU:0, one launch (start us, length us, event | category | flops | bytes accessed | tf_op | source)
XLA Modules:
  0.0 116.2 jit_solution(16794393230295813274)
XLA Ops:
  6.5 0.7 all-gather.2.cloned.1.call-update
  7.3 0.0 copy-start.1
  7.3 2.8 %copy-done.1 = bf16[1024,3072]{1,0:T(8,128)(2,1)S(1)} copy-done((bf16[1024,3072]{1,0:T(8,128)(2,1)S(1)}, bf16[1024,3072]{1,0:T(8,128)(2,1)}, u32[]{:S(2)}) %copy-start.1) | copy-done | bytes 6291480
  10.1 1.0 copy-done.2
  11.1 5.9 %own.1 = (bf16[2,1024,128]{2,1,0:T(8,128)(2,1)S(1)}, bf16[256,1024]{1,0:T(8,128)(2,1)S(1)}, bf16[2,1024,128]{2,1,0:T(8,128)(2,1)S(1)}) custom-call(bf16[256,1024]{1,0:T(8,128)(2,1)S(1)} %copy-done.2, bf16[1024,3072]{1,0:T(8,128)(2,1)S(1)} %copy-done.1), custom_call_target="tpu_custom_call" | custom-call | flops 1610612736 | bytes 6291456 | tf_op jit(solution)/shard_map/own/pallas_call | solution.py:49
  17.0 0.0 copy-start.16
  17.0 0.8 copy-done.16
  17.8 0.8 copy-done.19
  18.6 3.0 %collective-permute-start = (bf16[2,1024,128]{2,1,0:T(8,128)(2,1)S(1)}, bf16[2,1024,128]{2,1,0:T(8,128)(2,1)}, u32[]{:S(2)}, u32[]{:S(2)}) collective-permute-start(bf16[2,1024,128]{2,1,0:T(8,128)(2,1)S(1)} %get-tuple-element.30.q_ref), channel_id=1, source_target_pairs={{0,1},{1,0},{2,3},{3,2},{4,5},{5,4},{6,7},{7,6},{8,9},{9,8},{10,11... | collective-permute-start | bytes 1572872 | tf_op jit(solution)/shard_map/ppermute | solution.py:241
  21.6 1.5 %collective-permute-start.2 = (bf16[2,1024,128]{2,1,0:T(8,128)(2,1)S(1)}, bf16[2,1024,128]{2,1,0:T(8,128)(2,1)}, u32[]{:S(2)}, u32[]{:S(2)}) collective-permute-start(bf16[2,1024,128]{2,1,0:T(8,128)(2,1)S(1)} %get-tuple-element.30.q_ref), channel_id=1, source_target_pairs={{0,2},{1,3},{2,0},{3,1},{4,6},{5,7},{6,4},{7,5},{8,10},{9,11},{10,... | collective-permute-start | bytes 1572872 | tf_op jit(solution)/shard_map/ppermute | solution.py:241
  23.1 0.0 collective-permute-start.4
  23.1 0.1 copy.11
  23.2 0.1 iota_add_fusion.1
  23.3 0.1 add.111
  23.4 0.6 gather_fusion.1
  23.9 0.6 gather_fusion
  24.6 0.1 iota_add_fusion
  24.7 0.1 add.105
  24.8 0.1 fusion
  24.8 0.3 compare_reduce_fusion
  25.2 0.2 compare_reduce_fusion.1
  25.4 8.7 %copy.12 = bf16[1024,3072]{0,1:T(8,128)(2,1)} copy(bf16[1024,3072]{1,0:T(8,128)(2,1)} %w_ref.1) | data formatting | bytes 12582912 | tf_op args[1]
  34.0 0.0 copy-done.10
  34.0 0.1 select_n.40.flags
  34.1 0.1 copy.13
  34.2 0.1 reshape.129.flags
  34.3 4.4 %fusion.3 = (bf16[16,1,64,1024]{3,2,1,0:T(8,128)(2,1)S(1)}, bf16[16,1,64,1024]{3,2,1,0:T(8,128)(2,1)}) fusion(bf16[16,3,64,1024]{3,2,1,0:T(8,128)(2,1)} %bitcast.9), kind=kLoop, calls=%fused_computation.20 | loop fusion | bytes 8388608 | tf_op jit(solution)/shard_map/slice | solution.py:246
  38.7 0.0 collective-permute-done.q_ref
  38.7 2.9 %attend_near.5 = (f32[2,1024,128]{2,1,0:T(8,128)S(1)}, f32[2,8,256]{2,1,0:T(8,128)S(1)}, f32[2,8,256]{2,1,0:T(8,128)S(1)}) custom-call(s32[16]{0:T(128)S(1)} %reshape.129.flags, bf16[2,1024,128]{2,1,0:T(8,128)(2,1)} %collective-permute-done.q_ref, bf16[256,1024]{1,0:T(8,128)(2,1)S(1)} %copy-done.17, bf16[2,1024,128]{2,1,0:T(8,128)(2,1)S(1)} %copy-done.20), custom_call_target="tpu_custom_call" | custom-call | flops 536870912 | bytes 1048576 | tf_op jit(solution)/shard_map/attend_near/pallas_call | solution.py:175
  41.6 1.0 copy-done.8
  42.6 3.7 %collective-permute-done.2.q_ref = bf16[2,1024,128]{2,1,0:T(8,128)(2,1)} collective-permute-done((bf16[2,1024,128]{2,1,0:T(8,128)(2,1)S(1)}, bf16[2,1024,128]{2,1,0:T(8,128)(2,1)}, u32[]{:S(2)}, u32[]{:S(2)}) %collective-permute-start.2) | collective-permute-done | bytes 524320 | tf_op jit(solution)/shard_map/ppermute | solution.py:241
  46.3 2.3 %attend_near.6 = (f32[2,1024,128]{2,1,0:T(8,128)S(1)}, f32[2,8,256]{2,1,0:T(8,128)S(1)}, f32[2,8,256]{2,1,0:T(8,128)S(1)}) custom-call(s32[16]{0:T(128)S(1)} %reshape.129.flags, bf16[2,1024,128]{2,1,0:T(8,128)(2,1)} %collective-permute-done.2.q_ref, bf16[256,1024]{1,0:T(8,128)(2,1)S(1)} %copy-done.17, bf16[2,1024,128]{2,1,0:T(8,128)(2,1)S(1)} %copy-done.20), custom_call_target="tpu_custom_call" | custom-call | flops 536870912 | bytes 1048576 | tf_op jit(solution)/shard_map/attend_near/pallas_call | solution.py:175
  48.7 0.0 copy-start.6
  48.7 1.0 copy-done.6
  49.6 0.0 collective-permute-done.4.q_ref
  49.6 0.8 copy-done.12
  50.4 1.0 copy-done.13
  51.5 2.6 %attend_near.7 = (f32[2,1024,128]{2,1,0:T(8,128)S(1)}, f32[2,8,256]{2,1,0:T(8,128)S(1)}, f32[2,8,256]{2,1,0:T(8,128)S(1)}) custom-call(s32[16]{0:T(128)S(1)} %reshape.129.flags, bf16[2,1024,128]{2,1,0:T(8,128)(2,1)S(1)} %copy-done.13, bf16[256,1024]{1,0:T(8,128)(2,1)S(1)} %copy-done.17, bf16[2,1024,128]{2,1,0:T(8,128)(2,1)S(1)} %copy-done.20), custom_call_target="tpu_custom_call" | custom-call | flops 536870912 | bytes 1048576 | tf_op jit(solution)/shard_map/attend_near/pallas_call | solution.py:175
  54.1 4.6 %all-gather.2.cloned.1.call-done.x_ref = bf16[2048,1024]{1,0:T(8,128)(2,1)} async-done(((bf16[256,1024]{1,0:T(8,128)(2,1)}), bf16[2048,1024]{1,0:T(8,128)(2,1)}) %all-gather.2.cloned.1.call-update) | async-done | bytes 4194320 | tf_op jit(solution)/shard_map/all_gather | solution.py:236
  58.6 1.6 %copy-done.5 = bf16[16,1,64,1024]{3,2,1,0:T(8,128)(2,1)S(1)} copy-done((bf16[16,1,64,1024]{3,2,1,0:T(8,128)(2,1)S(1)}, bf16[16,1,64,1024]{3,2,1,0:T(8,128)(2,1)}, u32[]{:S(2)}) %copy-start.5) | copy-done | bytes 2097176
  60.2 2.2 %copy-done.15 = bf16[2048,1024]{1,0:T(8,128)(2,1)S(1)} copy-done((bf16[2048,1024]{1,0:T(8,128)(2,1)S(1)}, bf16[2048,1024]{1,0:T(8,128)(2,1)}, u32[]{:S(2)}) %copy-start.15) | copy-done | bytes 4194328
  62.4 10.4 %key_value.1 = (bf16[2048,1024]{1,0:T(8,128)(2,1)S(1)}, bf16[16,1024,128]{2,1,0:T(8,128)(2,1)S(1)}) custom-call(bf16[2048,1024]{1,0:T(8,128)(2,1)S(1)} %copy-done.15, bf16[1024,1024]{1,0:T(8,128)(2,1)S(1)} %bitcast.8, bf16[1024,1024]{1,0:T(8,128)(2,1)S(1)} %bitcast.7), custom_call_target="tpu_custom_call" | custom-call | flops 8589934592 | bytes 16777216 | tf_op jit(solution)/shard_map/key_value/pallas_call | solution.py:66
  72.8 0.0 copy-done.9
  72.8 0.0 copy-start.7
  72.8 2.9 %attend_far.5 = (bf16[2,1024,128]{2,1,0:T(8,128)(2,1)S(1)}, f32[2,2,8,256]{3,2,1,0:T(8,128)S(1)}) custom-call(s32[128]{0:T(128)S(1)} %select_n.40.flags, bf16[2,1024,128]{2,1,0:T(8,128)(2,1)} %collective-permute-done.q_ref, bf16[2048,1024]{1,0:T(8,128)(2,1)S(1)} %get-tuple-element.31.k_ref, bf16[16,1024,128]{2,1,0:T(8,128)(2,1)S(1)} %get-tuple-element.32.v_ref, ...), custom_call_target="tpu_custom_call" | custom-call | flops 536870912 | bytes 8388608 | tf_op jit(solution)/shard_map/attend_far/pallas_call | solution.py:175
  75.7 1.0 collective-permute-start.1
  76.6 2.3 %attend_far.6 = (bf16[2,1024,128]{2,1,0:T(8,128)(2,1)S(1)}, f32[2,2,8,256]{3,2,1,0:T(8,128)S(1)}) custom-call(s32[128]{0:T(128)S(1)} %select_n.40.flags, bf16[2,1024,128]{2,1,0:T(8,128)(2,1)} %collective-permute-done.2.q_ref, bf16[2048,1024]{1,0:T(8,128)(2,1)S(1)} %get-tuple-element.31.k_ref, bf16[16,1024,128]{2,1,0:T(8,128)(2,1)S(1)} %get-tuple-element.32.v_ref, ...), custom_call_target="tpu_custom_call" | custom-call | flops 536870912 | bytes 8388608 | tf_op jit(solution)/shard_map/attend_far/pallas_call | solution.py:175
  78.9 5.0 %collective-permute-start.3 = (bf16[2,1024,128]{2,1,0:T(8,128)(2,1)S(1)}, bf16[2,1024,128]{2,1,0:T(8,128)(2,1)S(1)}, u32[]{:S(2)}, u32[]{:S(2)}) collective-permute-start(bf16[2,1024,128]{2,1,0:T(8,128)(2,1)S(1)} %get-tuple-element.46), channel_id=1, source_target_pairs={{0,2},{1,3},{2,0},{3,1},{4,6},{5,7},{6,4},{7,5},{8,10},{9,11},{10,... | collective-permute-start | bytes 1572872 | tf_op jit(solution)/shard_map/ppermute | solution.py:241
  83.9 0.0 copy-done.14
  83.9 1.9 %attend_far.7 = (bf16[2,1024,128]{2,1,0:T(8,128)(2,1)S(1)}, f32[2,2,8,256]{3,2,1,0:T(8,128)S(1)}) custom-call(s32[128]{0:T(128)S(1)} %select_n.40.flags, bf16[2,1024,128]{2,1,0:T(8,128)(2,1)S(1)} %copy-done.14, bf16[2048,1024]{1,0:T(8,128)(2,1)S(1)} %get-tuple-element.31.k_ref, bf16[16,1024,128]{2,1,0:T(8,128)(2,1)S(1)} %get-tuple-element.32.v_ref, ...), custom_call_target="tpu_custom_call" | custom-call | flops 536870912 | bytes 8388608 | tf_op jit(solution)/shard_map/attend_far/pallas_call | solution.py:175
  85.8 0.1 collective-permute-start.5
  85.9 1.5 %collective-permute-start.6 = (f32[2,2,8,256]{3,2,1,0:T(8,128)S(1)}, f32[2,2,8,256]{3,2,1,0:T(8,128)S(1)}, u32[]{:S(2)}, u32[]{:S(2)}) collective-permute-start(f32[2,2,8,256]{3,2,1,0:T(8,128)S(1)} %get-tuple-element.52), channel_id=1, source_target_pairs={{0,1},{1,0},{2,3},{3,2},{4,5},{5,4},{6,7},{7,6},{8,9},{9,8},{10,11... | collective-permute-start | bytes 98312 | tf_op jit(solution)/shard_map/ppermute | solution.py:241
  87.4 0.0 copy-done.11
  87.4 3.2 %attend_near.4 = (f32[2,1024,128]{2,1,0:T(8,128)S(1)}, f32[2,8,256]{2,1,0:T(8,128)S(1)}, f32[2,8,256]{2,1,0:T(8,128)S(1)}) custom-call(s32[16]{0:T(128)S(1)} %reshape.129.flags, bf16[2,1024,128]{2,1,0:T(8,128)(2,1)S(1)} %copy-done.11, bf16[256,1024]{1,0:T(8,128)(2,1)S(1)} %copy-done.18, bf16[2,1024,128]{2,1,0:T(8,128)(2,1)S(1)} %copy-done.21), custom_call_target="tpu_custom_call" | custom-call | flops 536870912 | bytes 1048576 | tf_op jit(solution)/shard_map/attend_near/pallas_call | solution.py:175
  90.6 0.9 collective-permute-start.7
  91.4 10.9 %collective-permute-done.6.refs_7_ = f32[2,2,8,256]{3,2,1,0:T(8,128)S(1)} collective-permute-done((f32[2,2,8,256]{3,2,1,0:T(8,128)S(1)}, f32[2,2,8,256]{3,2,1,0:T(8,128)S(1)}, u32[]{:S(2)}, u32[]{:S(2)}) %collective-permute-start.6) | collective-permute-done | bytes 32800 | tf_op jit(solution)/shard_map/ppermute | solution.py:241
  102.3 1.9 %collective-permute-start.8 = (f32[2,2,8,256]{3,2,1,0:T(8,128)S(1)}, f32[2,2,8,256]{3,2,1,0:T(8,128)S(1)}, u32[]{:S(2)}, u32[]{:S(2)}) collective-permute-start(f32[2,2,8,256]{3,2,1,0:T(8,128)S(1)} %get-tuple-element.54), channel_id=1, source_target_pairs={{0,3},{1,2},{2,1},{3,0},{4,7},{5,6},{6,5},{7,4},{8,11},{9,10},{10,... | collective-permute-start | bytes 98312 | tf_op jit(solution)/shard_map/ppermute | solution.py:241
  104.2 1.9 %attend_far.4 = (bf16[2,1024,128]{2,1,0:T(8,128)(2,1)S(1)}, f32[2,2,8,256]{3,2,1,0:T(8,128)S(1)}) custom-call(s32[128]{0:T(128)S(1)} %select_n.40.flags, bf16[2,1024,128]{2,1,0:T(8,128)(2,1)S(1)} %copy-done.11, bf16[2048,1024]{1,0:T(8,128)(2,1)S(1)} %get-tuple-element.31.k_ref, bf16[16,1024,128]{2,1,0:T(8,128)(2,1)S(1)} %get-tuple-element.32.v_ref, ...), custom_call_target="tpu_custom_call" | custom-call | flops 536870912 | bytes 8388608 | tf_op jit(solution)/shard_map/attend_far/pallas_call | solution.py:175
  106.1 1.1 collective-permute-done.7.refs_8_
  107.2 0.0 collective-permute-done.8.refs_9_
  107.2 0.0 collective-permute-done.1.refs_3_
  107.2 0.0 collective-permute-done.3.refs_4_
  107.2 0.0 collective-permute-done.5.refs_5_
  107.2 2.2 %finish.1 = bf16[256,1024]{1,0:T(8,128)(2,1)} custom-call(bf16[256,1024]{1,0:T(8,128)(2,1)S(1)} %copy-done.3, bf16[1024,1024]{1,0:T(8,128)(2,1)S(1)} %copy-done.4, bf16[2,1024,128]{2,1,0:T(8,128)(2,1)S(1)} %get-tuple-element.38.refs_2_, bf16[2,1024,128]{2,1,0:T(8,128)(2,1)S(1)} %collective-permute-done.1.refs_3_, ...), custom_call_target="tpu_custom_call" | custom-call | tf_op jit(solution)/shard_map/finish/pallas_call | solution.py:216
  (37 shorter events, 0.1 us)
Async XLA Ops:
  6.5 17.4 %copy-start = (s32[64]{0:T(128)S(1)}, s32[64]{0:T(128)}, u32[]{:S(2)}) copy-start(s32[64]{0:T(128)} %param.9) | copy-start | bytes 772
  6.5 16.6 %copy-start.22 = (s32[64,32]{0,1:T(8,128)S(1)}, s32[64,32]{0,1:T(8,128)}, u32[]{:S(2)}) copy-start(s32[64,32]{0,1:T(8,128)} %param.8) | copy-start | bytes 24580
  6.5 52.1 %all-gather.2.cloned.1.call-start = ((), (), s32[]{:S(2)}) async-start(), calls=%async_computation | async-start | bytes 4718592 | tf_op jit(solution)/shard_map/all_gather | solution.py:236
  7.3 2.8 %copy-start.1 = (bf16[1024,3072]{1,0:T(8,128)(2,1)S(1)}, bf16[1024,3072]{1,0:T(8,128)(2,1)}, u32[]{:S(2)}) copy-start(bf16[1024,3072]{1,0:T(8,128)(2,1)} %w_ref.1) | copy-start | bytes 18874372
  10.0 1.0 copy-start.2
  17.0 0.8 copy-start.16
  17.8 0.8 copy-start.19
  18.6 15.4 %copy-start.10 = (bf16[2,1024,128]{2,1,0:T(8,128)(2,1)}, bf16[2,1024,128]{2,1,0:T(8,128)(2,1)S(1)}, u32[]{:S(2)}) copy-start(bf16[2,1024,128]{2,1,0:T(8,128)(2,1)S(1)} %get-tuple-element.30.q_ref) | copy-start | bytes 1572868
  18.6 20.0 %collective-permute-start = (bf16[2,1024,128]{2,1,0:T(8,128)(2,1)S(1)}, bf16[2,1024,128]{2,1,0:T(8,128)(2,1)}, u32[]{:S(2)}, u32[]{:S(2)}) collective-permute-start(bf16[2,1024,128]{2,1,0:T(8,128)(2,1)S(1)} %get-tuple-element.30.q_ref), channel_id=1, source_target_pairs={{0,1},{1,0},{2,3},{3,2},{4,5},{5,4},{6,7},{7,6},{8,9},{9,8},{10,11... | collective-permute-start | bytes 1572872 | tf_op jit(solution)/shard_map/ppermute | solution.py:241
  21.6 24.7 %collective-permute-start.2 = (bf16[2,1024,128]{2,1,0:T(8,128)(2,1)S(1)}, bf16[2,1024,128]{2,1,0:T(8,128)(2,1)}, u32[]{:S(2)}, u32[]{:S(2)}) collective-permute-start(bf16[2,1024,128]{2,1,0:T(8,128)(2,1)S(1)} %get-tuple-element.30.q_ref), channel_id=1, source_target_pairs={{0,2},{1,3},{2,0},{3,1},{4,6},{5,7},{6,4},{7,5},{8,10},{9,11},{10,... | collective-permute-start | bytes 1572872 | tf_op jit(solution)/shard_map/ppermute | solution.py:241
  23.1 26.5 %collective-permute-start.4 = (bf16[2,1024,128]{2,1,0:T(8,128)(2,1)S(1)}, bf16[2,1024,128]{2,1,0:T(8,128)(2,1)S(1)}, u32[]{:S(2)}, u32[]{:S(2)}) collective-permute-start(bf16[2,1024,128]{2,1,0:T(8,128)(2,1)S(1)} %get-tuple-element.30.q_ref), channel_id=1, source_target_pairs={{0,3},{1,2},{2,1},{3,0},{4,7},{5,6},{6,5},{7,4},{8,11},{9,10},{10,... | collective-permute-start | bytes 1572872 | tf_op jit(solution)/shard_map/ppermute | solution.py:241
  34.3 4.4 %copy-start.17 = (bf16[256,1024]{1,0:T(8,128)(2,1)S(1)}, bf16[256,1024]{1,0:T(8,128)(2,1)}, u32[]{:S(2)}) copy-start(bf16[256,1024]{1,0:T(8,128)(2,1)} %copy-done.16) | copy-start | bytes 1572868
  34.3 4.4 %copy-start.20 = (bf16[2,1024,128]{2,1,0:T(8,128)(2,1)S(1)}, bf16[2,1024,128]{2,1,0:T(8,128)(2,1)}, u32[]{:S(2)}) copy-start(bf16[2,1024,128]{2,1,0:T(8,128)(2,1)} %copy-done.19) | copy-start | bytes 1572868
  41.6 1.0 copy-start.8
  48.7 1.0 copy-start.6
  49.6 0.8 copy-start.12
  50.4 1.0 copy-start.13
  58.6 1.6 %copy-start.5 = (bf16[16,1,64,1024]{3,2,1,0:T(8,128)(2,1)S(1)}, bf16[16,1,64,1024]{3,2,1,0:T(8,128)(2,1)}, u32[]{:S(2)}) copy-start(bf16[16,1,64,1024]{3,2,1,0:T(8,128)(2,1)} %get-tuple-element.56) | copy-start | bytes 6291460
  60.2 2.2 %copy-start.15 = (bf16[2048,1024]{1,0:T(8,128)(2,1)S(1)}, bf16[2048,1024]{1,0:T(8,128)(2,1)}, u32[]{:S(2)}) copy-start(bf16[2048,1024]{1,0:T(8,128)(2,1)} %all-gather.2.cloned.1.call-done.x_ref) | copy-start | bytes 12582916
  62.4 10.4 %copy-start.9 = (f32[2,1024,128]{2,1,0:T(8,128)S(1)}, f32[2,1024,128]{2,1,0:T(8,128)}, u32[]{:S(2)}) copy-start(f32[2,1024,128]{2,1,0:T(8,128)} %copy-done.8) | copy-start | bytes 3145732
  72.8 3.8 %copy-start.7 = (f32[2,1024,128]{2,1,0:T(8,128)S(1)}, f32[2,1024,128]{2,1,0:T(8,128)}, u32[]{:S(2)}) copy-start(f32[2,1024,128]{2,1,0:T(8,128)} %copy-done.6) | copy-start | bytes 3145732
  75.7 31.5 %collective-permute-start.1 = (bf16[2,1024,128]{2,1,0:T(8,128)(2,1)S(1)}, bf16[2,1024,128]{2,1,0:T(8,128)(2,1)S(1)}, u32[]{:S(2)}, u32[]{:S(2)}) collective-permute-start(bf16[2,1024,128]{2,1,0:T(8,128)(2,1)S(1)} %get-tuple-element.42), channel_id=1, source_target_pairs={{0,1},{1,0},{2,3},{3,2},{4,5},{5,4},{6,7},{7,6},{8,9},{9,8},{10,11... | collective-permute-start | bytes 1572872 | tf_op jit(solution)/shard_map/ppermute | solution.py:241
  76.6 7.2 %copy-start.14 = (bf16[2,1024,128]{2,1,0:T(8,128)(2,1)S(1)}, bf16[2,1024,128]{2,1,0:T(8,128)(2,1)}, u32[]{:S(2)}) copy-start(bf16[2,1024,128]{2,1,0:T(8,128)(2,1)} %copy-done.12) | copy-start | bytes 1572868
  78.9 28.3 %collective-permute-start.3 = (bf16[2,1024,128]{2,1,0:T(8,128)(2,1)S(1)}, bf16[2,1024,128]{2,1,0:T(8,128)(2,1)S(1)}, u32[]{:S(2)}, u32[]{:S(2)}) collective-permute-start(bf16[2,1024,128]{2,1,0:T(8,128)(2,1)S(1)} %get-tuple-element.46), channel_id=1, source_target_pairs={{0,2},{1,3},{2,0},{3,1},{4,6},{5,7},{6,4},{7,5},{8,10},{9,11},{10,... | collective-permute-start | bytes 1572872 | tf_op jit(solution)/shard_map/ppermute | solution.py:241
  83.9 3.5 %copy-start.11 = (bf16[2,1024,128]{2,1,0:T(8,128)(2,1)S(1)}, bf16[2,1024,128]{2,1,0:T(8,128)(2,1)}, u32[]{:S(2)}) copy-start(bf16[2,1024,128]{2,1,0:T(8,128)(2,1)} %copy-done.10) | copy-start | bytes 1572868
  83.9 3.5 %copy-start.18 = (bf16[256,1024]{1,0:T(8,128)(2,1)S(1)}, bf16[256,1024]{1,0:T(8,128)(2,1)}, u32[]{:S(2)}) copy-start(bf16[256,1024]{1,0:T(8,128)(2,1)} %copy-done.16) | copy-start | bytes 1572868
  83.9 3.5 %copy-start.21 = (bf16[2,1024,128]{2,1,0:T(8,128)(2,1)S(1)}, bf16[2,1024,128]{2,1,0:T(8,128)(2,1)}, u32[]{:S(2)}) copy-start(bf16[2,1024,128]{2,1,0:T(8,128)(2,1)} %copy-done.19) | copy-start | bytes 1572868
  85.8 21.4 %collective-permute-start.5 = (bf16[2,1024,128]{2,1,0:T(8,128)(2,1)S(1)}, bf16[2,1024,128]{2,1,0:T(8,128)(2,1)S(1)}, u32[]{:S(2)}, u32[]{:S(2)}) collective-permute-start(bf16[2,1024,128]{2,1,0:T(8,128)(2,1)S(1)} %get-tuple-element.50), channel_id=1, source_target_pairs={{0,3},{1,2},{2,1},{3,0},{4,7},{5,6},{6,5},{7,4},{8,11},{9,10},{10,... | collective-permute-start | bytes 1572872 | tf_op jit(solution)/shard_map/ppermute | solution.py:241
  85.9 16.4 %collective-permute-start.6 = (f32[2,2,8,256]{3,2,1,0:T(8,128)S(1)}, f32[2,2,8,256]{3,2,1,0:T(8,128)S(1)}, u32[]{:S(2)}, u32[]{:S(2)}) collective-permute-start(f32[2,2,8,256]{3,2,1,0:T(8,128)S(1)} %get-tuple-element.52), channel_id=1, source_target_pairs={{0,1},{1,0},{2,3},{3,2},{4,5},{5,4},{6,7},{7,6},{8,9},{9,8},{10,11... | collective-permute-start | bytes 98312 | tf_op jit(solution)/shard_map/ppermute | solution.py:241
  90.6 16.6 %collective-permute-start.7 = (f32[2,2,8,256]{3,2,1,0:T(8,128)S(1)}, f32[2,2,8,256]{3,2,1,0:T(8,128)S(1)}, u32[]{:S(2)}, u32[]{:S(2)}) collective-permute-start(f32[2,2,8,256]{3,2,1,0:T(8,128)S(1)} %get-tuple-element.53), channel_id=1, source_target_pairs={{0,2},{1,3},{2,0},{3,1},{4,6},{5,7},{6,4},{7,5},{8,10},{9,11},{10,... | collective-permute-start | bytes 98312 | tf_op jit(solution)/shard_map/ppermute | solution.py:241
  102.3 4.8 %collective-permute-start.8 = (f32[2,2,8,256]{3,2,1,0:T(8,128)S(1)}, f32[2,2,8,256]{3,2,1,0:T(8,128)S(1)}, u32[]{:S(2)}, u32[]{:S(2)}) collective-permute-start(f32[2,2,8,256]{3,2,1,0:T(8,128)S(1)} %get-tuple-element.54), channel_id=1, source_target_pairs={{0,3},{1,2},{2,1},{3,0},{4,7},{5,6},{6,5},{7,4},{8,11},{9,10},{10,... | collective-permute-start | bytes 98312 | tf_op jit(solution)/shard_map/ppermute | solution.py:241
  104.2 3.0 %copy-start.3 = (bf16[256,1024]{1,0:T(8,128)(2,1)S(1)}, bf16[256,1024]{1,0:T(8,128)(2,1)}, u32[]{:S(2)}) copy-start(bf16[256,1024]{1,0:T(8,128)(2,1)} %refs_0_.1) | copy-start | bytes 1572868
  104.2 3.0 %copy-start.4 = (bf16[1024,1024]{1,0:T(8,128)(2,1)S(1)}, bf16[1024,1024]{1,0:T(8,128)(2,1)}, u32[]{:S(2)}) copy-start(bf16[1024,1024]{1,0:T(8,128)(2,1)} %refs_1_.1) | copy-start | bytes 6291460
Sparse Core Ops, SparseCore 0:
  8.9 49.6 all-gather.1

commit v3 on v2

--- a/solution.py
+++ b/solution.py
@@ -18,10 +18,15 @@
 VMEM_LIMIT = 20 * MIB
 
 
-def own_kernel(x_ref, w_ref, q_ref, k_ref, v_ref):
+def own_kernel(x_ref, w_ref, q_ref, k_ref, v_ref, wk_ref, wv_ref):
     y = jnp.dot(x_ref[...], w_ref[...], preferred_element_type=jnp.float32)
     turned = y.T
     e = HEAD_DIM
+    w = w_ref[...].T
+    for i in range(2):
+        at = 3 * e * i
+        wk_ref[i * e : (i + 1) * e, :] = w[at + e : at + 2 * e]
+        wv_ref[i * e : (i + 1) * e, :] = w[at + 2 * e : at + 3 * e]
     q = jnp.concatenate([turned[:e], turned[3 * e : 4 * e]], axis=0).astype(jnp.bfloat16)
     q = q * jnp.bfloat16(HEAD_DIM ** -0.5)
     k = jnp.concatenate([turned[e : 2 * e], turned[4 * e : 5 * e]], axis=0)
@@ -32,7 +37,7 @@
         v_ref[j] = v[:, j * TILE : (j + 1) * TILE]
 
 
-def key_value_kernel(x_ref, wk_ref, wv_ref, k_ref, v_ref):
+def key_value_kernel(skip, x_ref, wk_ref, wv_ref, k_ref, v_ref):
     x = x_ref[...]
     k = lax.dot_general(x, wk_ref[...], TRANSPOSED, preferred_element_type=jnp.float32)
     v = lax.dot_general(wv_ref[...], x, TRANSPOSED, preferred_element_type=jnp.float32)
@@ -53,28 +58,33 @@
             pl.BlockSpec((rows, width), lambda p: (0, 0)),
             pl.BlockSpec((width, 3 * PAIR), lambda p: (0, p)),
         ],
-        out_specs=[turned_spec, pl.BlockSpec((rows, PAIR), lambda p: (0, p)), turned_spec],
-        out_shape=[turned, jax.ShapeDtypeStruct((rows, width), jnp.bfloat16), turned],
+        out_specs=[turned_spec, pl.BlockSpec((rows, PAIR), lambda p: (0, p)), turned_spec]
+        + [pl.BlockSpec((PAIR, width), lambda p: (p, 0))] * 2,
+        out_shape=[turned, jax.ShapeDtypeStruct((rows, width), jnp.bfloat16), turned]
+        + [jax.ShapeDtypeStruct((width, width), jnp.bfloat16)] * 2,
         compiler_params=pltpu.CompilerParams(vmem_limit_bytes=16 * 1024 * 1024),
         cost_estimate=pl.CostEstimate(flops=6 * rows * width * width, bytes_accessed=6 * width * width, transcendentals=0),
         name="own",
     )(x, w)
 
 
-def project_key_value(x, wk, wv, step):
+def project_key_value(skip, x, wk, wv, step):
     rows, width = x.shape
     return pl.pallas_call(
         key_value_kernel,
-        grid=(rows // step,),
-        in_specs=[
-            pl.BlockSpec((step, width), lambda i: (i, 0)),
-            pl.BlockSpec((width, width), lambda i: (0, 0)),
-            pl.BlockSpec((width, width), lambda i: (0, 0)),
-        ],
-        out_specs=[
-            pl.BlockSpec((step, width), lambda i: (i, 0)),
-            pl.BlockSpec((step // TILE, width, TILE), lambda i: (i, 0, 0)),
-        ],
+        grid_spec=pltpu.PrefetchScalarGridSpec(
+            num_scalar_prefetch=1,
+            grid=(rows // step - 1,),
+            in_specs=[
+                pl.BlockSpec((step, width), lambda i, g: (i + (i >= g[0]).astype(jnp.int32), 0)),
+                pl.BlockSpec((width, width), lambda i, g: (0, 0)),
+                pl.BlockSpec((width, width), lambda i, g: (0, 0)),
+            ],
+            out_specs=[
+                pl.BlockSpec((step, width), lambda i, g: (i + (i >= g[0]).astype(jnp.int32), 0)),
+                pl.BlockSpec((step // TILE, width, TILE), lambda i, g: (i + (i >= g[0]).astype(jnp.int32), 0, 0)),
+            ],
+        ),
         out_shape=[
             jax.ShapeDtypeStruct((rows, width), jnp.bfloat16),
             jax.ShapeDtypeStruct((rows // TILE, width, TILE), jnp.bfloat16),
@@ -84,7 +94,7 @@
             flops=4 * rows * width * width, bytes_accessed=6 * rows * width + 4 * width * width, transcendentals=0
         ),
         name="key_value",
-    )(x, wk, wv)
+    )(skip, x, wk, wv)
 
 
 def attend_kernel(first, offset, key_tiles, flags, q_ref, k_ref, v_ref, *rest):
@@ -240,11 +250,8 @@
             return value
         return lax.ppermute(value, "sp", [(i, i ^ k) for i in range(sp)])
 
-    q_own, k_own, v_own = project_own(nodes, project_in)
+    q_own, k_own, v_own, wk, wv = project_own(nodes, project_in)
     queries = [swap(k, q_own) for k in range(sp)]
-    weights = project_in.T.reshape(HEADS, 3, HEAD_DIM, width)
-    wk, wv = weights[:, 1].reshape(width, width), weights[:, 2].reshape(width, width)
-
     partner = s ^ jnp.arange(sp, dtype=jnp.int32)
     local = jnp.arange(own, dtype=jnp.int32)
     q_tiles = (g * group_tiles + partner[:, None] * own + local[None, :]).reshape(-1)
@@ -258,7 +265,7 @@
 
     near, distant = near.reshape(-1), distant.reshape(-1)
     states = [attend(near, k * own, queries[k], k_own, v_own) for k in range(sp)]
-    k_far, v_far = project_key_value(far, wk, wv, rows)
+    k_far, v_far = project_key_value(jnp.reshape(g, (1,)).astype(jnp.int32), far, wk, wv, rows)
     parts, stats = [None] * sp, [None] * sp
     for k in reversed(range(sp)):
         part, stat = attend(distant, k * own, queries[k], k_far, v_far, states[k])

time: 118 us -> 118 us (level); the launches traced: 116 us -> 118 us
  waiting for transfers between devices: 21 us -> 36.3 us
  local copies, waits for them, and re-layouts: 27.7 us -> 21.3 us
  Pallas kernels: 38.4 us -> 33.8 us
  starting transfers between devices: 14.7 us -> 11.8 us
    ppermute x9, waiting for transfers between devices: 15.7 us -> 35.6 us  [swap(): return lax.ppermute(value, 'sp', [(i, i ^ k) for i in range(sp)])]
    all_gather x1, waiting for transfers between devices: 4.58 us -> 0.02 us  [shards(): far = lax.all_gather(nodes, 'pb', axis=0, tiled=True)]
    slice x1 -> x0, local copies, waits for them, and re-layouts: 4.37 us -> none  [shards(): weights[:, 2].reshape(width, width)]
    pallas_call x8, Pallas kernels: 19.9 us -> 16.6 us  [attend(): pl.pallas_call(functools.partial(attend_kernel, first, offset, key_tiles)...]
    ppermute x9, starting transfers between devices: 14.7 us -> 11.8 us  [swap(): return lax.ppermute(value, 'sp', [(i, i ^ k) for i in range(sp)])]
    unnamed x48 -> x55, local copies, waits for them, and re-layouts: 21.8 us -> 19.6 us
    pallas_call x1, Pallas kernels: 10.4 us -> 9.07 us  [project_key_value(): pl.pallas_call(key_value_kernel, grid_spec=pltpu.PrefetchScalarGridSpec(n...]
  transfers between devices with their start and end apart: 10 -> 10, of which waited for: 4 -> 4; matrix products, arithmetic and copies ran while one was open for 13% -> 2% of each run, Pallas kernels for 20% -> 17%
where the time goes in v3:
time: 118 us
  waiting for transfers between devices  36.3 us (31%)
  Pallas kernels  33.8 us (29%)
  local copies, waits for them, and re-layouts  21.3 us (18%)
  between operations  13.7 us (12%)
  starting transfers between devices  11.8 us (10%)
    ppermute x9, waiting for transfers between devices, swap(): return lax.ppermute(value, 'sp', [(i, i ^ k) for i in range(sp)])  35.6 us
    unnamed x55, local copies, waits for them, and re-layouts  19.6 us
    pallas_call x8, Pallas kernels, attend(): pl.pallas_call(functools.partial(attend_kernel, first, offset, key_tiles)...  16.6 us
    ppermute x9, starting transfers between devices, swap(): return lax.ppermute(value, 'sp', [(i, i ^ k) for i in range(sp)])  11.8 us
    pallas_call x1, Pallas kernels, project_key_value(): pl.pallas_call(key_value_kernel, grid_spec=pltpu.PrefetchScalarGridSpec(n...  9.07 us
    pallas_call x1, Pallas kernels, project_own(): pl.pallas_call(own_kernel, grid=(PAIRS,), in_specs=[pl.BlockSpec((rows, w...  5.89 us
  transfers between devices with their start and end apart: 10, of which 4 were waited for; matrix products, arithmetic and copies ran while one was open for 2% of the time, Pallas kernels for 17%

profile of v3, /device:TPU:0, one launch (start us, length us, event | category | flops | bytes accessed | tf_op | source)
XLA Modules:
  0.0 117.6 jit_solution(7075943406759116843)
XLA Ops:
  6.5 0.7 all-gather.2.cloned.1.call-update
  7.3 2.8 %copy-done.1 = bf16[1024,3072]{1,0:T(8,128)(2,1)S(1)} copy-done((bf16[1024,3072]{1,0:T(8,128)(2,1)S(1)}, bf16[1024,3072]{1,0:T(8,128)(2,1)}, u32[]{:S(2)}) %copy-start.1) | copy-done | bytes 6291480
  10.0 1.0 copy-done.2
  11.1 5.9 %own.1 = (bf16[2,1024,128]{2,1,0:T(8,128)(2,1)S(1)}, bf16[256,1024]{1,0:T(8,128)(2,1)S(1)}, bf16[2,1024,128]{2,1,0:T(8,128)(2,1)S(1)}, bf16[1024,1024]{1,0:T(8,128)(2,1)S(1)}, bf16[1024,1024]{1,0:T(8,128)(2,1)S(1)}) custom-call(bf16[256,1024]{1,0:T(8,128)(2,1)S(1)} %copy-done.2, bf16[1024,3072]{1,0:T(8,128)(2,1)S(1)} %copy-done.1), custom_call_target="tpu_custom_call" | custom-call | flops 1610612736 | bytes 6291456 | tf_op jit(solution)/shard_map/own/pallas_call | solution.py:54
  17.0 0.0 copy-start.16
  17.0 1.4 %copy-done.16 = bf16[1024,1024]{1,0:T(8,128)(2,1)} copy-done((bf16[1024,1024]{1,0:T(8,128)(2,1)}, bf16[1024,1024]{1,0:T(8,128)(2,1)S(1)}, u32[]{:S(2)}) %copy-start.16) | copy-done | bytes 2097176
  18.4 1.4 %copy-done.18 = bf16[1024,1024]{1,0:T(8,128)(2,1)} copy-done((bf16[1024,1024]{1,0:T(8,128)(2,1)}, bf16[1024,1024]{1,0:T(8,128)(2,1)S(1)}, u32[]{:S(2)}) %copy-start.18) | copy-done | bytes 2097176
  19.8 0.8 copy-done.20
  20.6 0.8 copy-done.23
  21.4 3.9 %collective-permute-start.4 = (bf16[2,1024,128]{2,1,0:T(8,128)(2,1)S(1)}, bf16[2,1024,128]{2,1,0:T(8,128)(2,1)S(1)}, u32[]{:S(2)}, u32[]{:S(2)}) collective-permute-start(bf16[2,1024,128]{2,1,0:T(8,128)(2,1)S(1)} %get-tuple-element.32.q_ref), channel_id=1, source_target_pairs={{0,3},{1,2},{2,1},{3,0},{4,7},{5,6},{6,5},{7,4},{8,11},{9,10},{10,... | collective-permute-start | bytes 1572872 | tf_op jit(solution)/shard_map/ppermute | solution.py:251
  25.3 0.5 collective-permute-start.2
  25.8 0.1 collective-permute-start
  25.9 0.1 iota_add_fusion.1
  26.0 0.1 add.111
  26.1 0.1 iota_add_fusion
  26.2 0.1 add.105
  26.2 0.1 copy.8
  26.3 0.6 gather_fusion
  27.0 0.6 gather_fusion.1
  27.6 0.1 fusion
  27.6 0.3 compare_reduce_fusion
  27.9 0.2 compare_reduce_fusion.1
  28.2 0.1 select_n.40.flags
  28.3 0.1 copy.9
  28.3 0.1 reshape.129.flags
  28.4 20.4 %collective-permute-done.q_ref = bf16[2,1024,128]{2,1,0:T(8,128)(2,1)S(1)} collective-permute-done((bf16[2,1024,128]{2,1,0:T(8,128)(2,1)S(1)}, bf16[2,1024,128]{2,1,0:T(8,128)(2,1)S(1)}, u32[]{:S(2)}, u32[]{:S(2)}) %collective-permute-start) | collective-permute-done | bytes 524320 | tf_op jit(solution)/shard_map/ppermute | solution.py:251
  48.8 1.2 %copy-done.21 = bf16[256,1024]{1,0:T(8,128)(2,1)S(1)} copy-done((bf16[256,1024]{1,0:T(8,128)(2,1)S(1)}, bf16[256,1024]{1,0:T(8,128)(2,1)}, u32[]{:S(2)}) %copy-start.21) | copy-done | bytes 524312
  50.0 1.0 copy-done.24
  51.1 0.8 attend_near.5
  51.9 0.0 copy-done.13
  51.9 0.0 collective-permute-done.2.q_ref
  51.9 0.8 copy-done.10
  52.7 1.0 copy-done.11
  53.8 0.8 attend_near.6
  54.6 0.0 collective-permute-done.4.q_ref
  54.6 0.0 copy-start.7
  54.6 0.8 copy-done.7
  55.4 1.0 copy-done.8
  56.4 3.1 %attend_near.7 = (f32[2,1024,128]{2,1,0:T(8,128)S(1)}, f32[2,8,256]{2,1,0:T(8,128)S(1)}, f32[2,8,256]{2,1,0:T(8,128)S(1)}) custom-call(s32[16]{0:T(128)S(1)} %reshape.129.flags, bf16[2,1024,128]{2,1,0:T(8,128)(2,1)S(1)} %copy-done.8, bf16[256,1024]{1,0:T(8,128)(2,1)S(1)} %copy-done.21, bf16[2,1024,128]{2,1,0:T(8,128)(2,1)S(1)} %copy-done.24), custom_call_target="tpu_custom_call" | custom-call | flops 536870912 | bytes 1048576 | tf_op jit(solution)/shard_map/attend_near/pallas_call | solution.py:185
  59.6 0.0 all-gather.2.cloned.1.call-done.x_ref
  59.6 2.2 %copy-done.15 = bf16[2048,1024]{1,0:T(8,128)(2,1)S(1)} copy-done((bf16[2048,1024]{1,0:T(8,128)(2,1)S(1)}, bf16[2048,1024]{1,0:T(8,128)(2,1)}, u32[]{:S(2)}) %copy-start.15) | copy-done | bytes 4194328
  61.8 1.6 %copy-done.17 = bf16[1024,1024]{1,0:T(8,128)(2,1)S(1)} copy-done((bf16[1024,1024]{1,0:T(8,128)(2,1)S(1)}, bf16[1024,1024]{1,0:T(8,128)(2,1)}, u32[]{:S(2)}) %copy-start.17) | copy-done | bytes 2097176
  63.4 1.6 %copy-done.19 = bf16[1024,1024]{1,0:T(8,128)(2,1)S(1)} copy-done((bf16[1024,1024]{1,0:T(8,128)(2,1)S(1)}, bf16[1024,1024]{1,0:T(8,128)(2,1)}, u32[]{:S(2)}) %copy-start.19) | copy-done | bytes 2097176
  65.0 9.1 %key_value.1 = (bf16[2048,1024]{1,0:T(8,128)(2,1)S(1)}, bf16[16,1024,128]{2,1,0:T(8,128)(2,1)S(1)}) custom-call(s32[1]{0:T(128)} %bitcast.1.skip, bf16[2048,1024]{1,0:T(8,128)(2,1)S(1)} %copy-done.15, bf16[1024,1024]{1,0:T(8,128)(2,1)S(1)} %copy-done.17, bf16[1024,1024]{1,0:T(8,128)(2,1)S(1)} %copy-done.19), custom_call_target="tpu_custom_call" | custom-call | flops 8589934592 | bytes 16777216 | tf_op jit(solution)/shard_map/key_value/pallas_call | solution.py:73
  74.0 0.0 copy-done.14
  74.0 0.0 copy-start.12
  74.1 3.1 %attend_far.5 = (bf16[2,1024,128]{2,1,0:T(8,128)(2,1)S(1)}, f32[2,2,8,256]{3,2,1,0:T(8,128)S(1)}) custom-call(s32[128]{0:T(128)S(1)} %select_n.40.flags, bf16[2,1024,128]{2,1,0:T(8,128)(2,1)S(1)} %copy-done.14, bf16[2048,1024]{1,0:T(8,128)(2,1)S(1)} %get-tuple-element.35.k_ref, bf16[16,1024,128]{2,1,0:T(8,128)(2,1)S(1)} %get-tuple-element.36.v_ref, ...), custom_call_target="tpu_custom_call" | custom-call | flops 536870912 | bytes 8388608 | tf_op jit(solution)/shard_map/attend_far/pallas_call | solution.py:185
  77.1 2.2 %collective-permute-start.1 = (bf16[2,1024,128]{2,1,0:T(8,128)(2,1)S(1)}, bf16[2,1024,128]{2,1,0:T(8,128)(2,1)S(1)}, u32[]{:S(2)}, u32[]{:S(2)}) collective-permute-start(bf16[2,1024,128]{2,1,0:T(8,128)(2,1)S(1)} %get-tuple-element.46), channel_id=1, source_target_pairs={{0,1},{1,0},{2,3},{3,2},{4,5},{5,4},{6,7},{7,6},{8,9},{9,8},{10,11... | collective-permute-start | bytes 1572872 | tf_op jit(solution)/shard_map/ppermute | solution.py:251
  79.3 1.3 %attend_far.6 = (bf16[2,1024,128]{2,1,0:T(8,128)(2,1)S(1)}, f32[2,2,8,256]{3,2,1,0:T(8,128)S(1)}) custom-call(s32[128]{0:T(128)S(1)} %select_n.40.flags, bf16[2,1024,128]{2,1,0:T(8,128)(2,1)S(1)} %copy-done.12, bf16[2048,1024]{1,0:T(8,128)(2,1)S(1)} %get-tuple-element.35.k_ref, bf16[16,1024,128]{2,1,0:T(8,128)(2,1)S(1)} %get-tuple-element.36.v_ref, ...), custom_call_target="tpu_custom_call" | custom-call | flops 536870912 | bytes 8388608 | tf_op jit(solution)/shard_map/attend_far/pallas_call | solution.py:185
  80.6 2.3 %collective-permute-start.3 = (bf16[2,1024,128]{2,1,0:T(8,128)(2,1)S(1)}, bf16[2,1024,128]{2,1,0:T(8,128)(2,1)S(1)}, u32[]{:S(2)}, u32[]{:S(2)}) collective-permute-start(bf16[2,1024,128]{2,1,0:T(8,128)(2,1)S(1)} %get-tuple-element.50), channel_id=1, source_target_pairs={{0,2},{1,3},{2,0},{3,1},{4,6},{5,7},{6,4},{7,5},{8,10},{9,11},{10,... | collective-permute-start | bytes 1572872 | tf_op jit(solution)/shard_map/ppermute | solution.py:251
  82.9 2.5 %attend_far.7 = (bf16[2,1024,128]{2,1,0:T(8,128)(2,1)S(1)}, f32[2,2,8,256]{3,2,1,0:T(8,128)S(1)}) custom-call(s32[128]{0:T(128)S(1)} %select_n.40.flags, bf16[2,1024,128]{2,1,0:T(8,128)(2,1)S(1)} %copy-done.9, bf16[2048,1024]{1,0:T(8,128)(2,1)S(1)} %get-tuple-element.35.k_ref, bf16[16,1024,128]{2,1,0:T(8,128)(2,1)S(1)} %get-tuple-element.36.v_ref, ...), custom_call_target="tpu_custom_call" | custom-call | flops 536870912 | bytes 8388608 | tf_op jit(solution)/shard_map/attend_far/pallas_call | solution.py:185
  85.4 1.1 collective-permute-start.5
  86.5 1.7 %collective-permute-start.6 = (f32[2,2,8,256]{3,2,1,0:T(8,128)S(1)}, f32[2,2,8,256]{3,2,1,0:T(8,128)S(1)}, u32[]{:S(2)}, u32[]{:S(2)}) collective-permute-start(f32[2,2,8,256]{3,2,1,0:T(8,128)S(1)} %get-tuple-element.56), channel_id=1, source_target_pairs={{0,1},{1,0},{2,3},{3,2},{4,5},{5,4},{6,7},{7,6},{8,9},{9,8},{10,11... | collective-permute-start | bytes 98312 | tf_op jit(solution)/shard_map/ppermute | solution.py:251
  88.2 3.1 %attend_near.4 = (f32[2,1024,128]{2,1,0:T(8,128)S(1)}, f32[2,8,256]{2,1,0:T(8,128)S(1)}, f32[2,8,256]{2,1,0:T(8,128)S(1)}) custom-call(s32[16]{0:T(128)S(1)} %reshape.129.flags, bf16[2,1024,128]{2,1,0:T(8,128)(2,1)S(1)} %copy-done.6, bf16[256,1024]{1,0:T(8,128)(2,1)S(1)} %copy-done.22, bf16[2,1024,128]{2,1,0:T(8,128)(2,1)S(1)} %copy-done.25), custom_call_target="tpu_custom_call" | custom-call | flops 536870912 | bytes 1048576 | tf_op jit(solution)/shard_map/attend_near/pallas_call | solution.py:185
  91.3 0.1 collective-permute-start.7
  91.4 12.3 %collective-permute-done.6.refs_7_ = f32[2,2,8,256]{3,2,1,0:T(8,128)S(1)} collective-permute-done((f32[2,2,8,256]{3,2,1,0:T(8,128)S(1)}, f32[2,2,8,256]{3,2,1,0:T(8,128)S(1)}, u32[]{:S(2)}, u32[]{:S(2)}) %collective-permute-start.6) | collective-permute-done | bytes 32800 | tf_op jit(solution)/shard_map/ppermute | solution.py:251
  103.7 0.0 collective-permute-start.8
  103.7 1.9 %attend_far.4 = (bf16[2,1024,128]{2,1,0:T(8,128)(2,1)S(1)}, f32[2,2,8,256]{3,2,1,0:T(8,128)S(1)}) custom-call(s32[128]{0:T(128)S(1)} %select_n.40.flags, bf16[2,1024,128]{2,1,0:T(8,128)(2,1)S(1)} %copy-done.6, bf16[2048,1024]{1,0:T(8,128)(2,1)S(1)} %get-tuple-element.35.k_ref, bf16[16,1024,128]{2,1,0:T(8,128)(2,1)S(1)} %get-tuple-element.36.v_ref, ...), custom_call_target="tpu_custom_call" | custom-call | flops 536870912 | bytes 8388608 | tf_op jit(solution)/shard_map/attend_far/pallas_call | solution.py:185
  105.6 2.1 %collective-permute-done.7.refs_8_ = f32[2,2,8,256]{3,2,1,0:T(8,128)S(1)} collective-permute-done((f32[2,2,8,256]{3,2,1,0:T(8,128)S(1)}, f32[2,2,8,256]{3,2,1,0:T(8,128)S(1)}, u32[]{:S(2)}, u32[]{:S(2)}) %collective-permute-start.7) | collective-permute-done | bytes 32800 | tf_op jit(solution)/shard_map/ppermute | solution.py:251
  107.6 0.9 collective-permute-done.8.refs_9_
  108.5 0.0 collective-permute-done.1.refs_3_
  108.5 0.0 collective-permute-done.3.refs_4_
  108.5 0.0 collective-permute-done.5.refs_5_
  108.5 2.2 %finish.1 = bf16[256,1024]{1,0:T(8,128)(2,1)} custom-call(bf16[256,1024]{1,0:T(8,128)(2,1)S(1)} %copy-done.3, bf16[1024,1024]{1,0:T(8,128)(2,1)S(1)} %copy-done.4, bf16[2,1024,128]{2,1,0:T(8,128)(2,1)S(1)} %get-tuple-element.42.refs_2_, bf16[2,1024,128]{2,1,0:T(8,128)(2,1)S(1)} %collective-permute-done.1.refs_3_, ...), custom_call_target="tpu_custom_call" | custom-call | tf_op jit(solution)/shard_map/finish/pallas_call | solution.py:226
  (43 shorter events, 0.1 us)
Async XLA Ops:
  6.5 19.8 %copy-start = (s32[64]{0:T(128)S(1)}, s32[64]{0:T(128)}, u32[]{:S(2)}) copy-start(s32[64]{0:T(128)} %param.9) | copy-start | bytes 772
  6.5 19.7 %copy-start.26 = (s32[64,32]{0,1:T(8,128)S(1)}, s32[64,32]{0,1:T(8,128)}, u32[]{:S(2)}) copy-start(s32[64,32]{0,1:T(8,128)} %param.8) | copy-start | bytes 24580
  6.5 53.0 %all-gather.2.cloned.1.call-start = ((), (), s32[]{:S(2)}) async-start(), calls=%async_computation | async-start | bytes 4718592 | tf_op jit(solution)/shard_map/all_gather | solution.py:246
  7.3 2.8 %copy-start.1 = (bf16[1024,3072]{1,0:T(8,128)(2,1)S(1)}, bf16[1024,3072]{1,0:T(8,128)(2,1)}, u32[]{:S(2)}) copy-start(bf16[1024,3072]{1,0:T(8,128)(2,1)} %w_ref.1) | copy-start | bytes 18874372
  10.0 1.0 copy-start.2
  17.0 1.4 %copy-start.16 = (bf16[1024,1024]{1,0:T(8,128)(2,1)}, bf16[1024,1024]{1,0:T(8,128)(2,1)S(1)}, u32[]{:S(2)}) copy-start(bf16[1024,1024]{1,0:T(8,128)(2,1)S(1)} %get-tuple-element.33.wk_ref) | copy-start | bytes 6291460
  18.4 1.4 %copy-start.18 = (bf16[1024,1024]{1,0:T(8,128)(2,1)}, bf16[1024,1024]{1,0:T(8,128)(2,1)S(1)}, u32[]{:S(2)}) copy-start(bf16[1024,1024]{1,0:T(8,128)(2,1)S(1)} %get-tuple-element.34.wv_ref) | copy-start | bytes 6291460
  19.8 0.8 copy-start.20
  20.6 0.8 copy-start.23
  21.4 33.2 %copy-start.5 = (bf16[2,1024,128]{2,1,0:T(8,128)(2,1)}, bf16[2,1024,128]{2,1,0:T(8,128)(2,1)S(1)}, u32[]{:S(2)}) copy-start(bf16[2,1024,128]{2,1,0:T(8,128)(2,1)S(1)} %get-tuple-element.32.q_ref) | copy-start | bytes 1572868
  21.4 33.2 %collective-permute-start.4 = (bf16[2,1024,128]{2,1,0:T(8,128)(2,1)S(1)}, bf16[2,1024,128]{2,1,0:T(8,128)(2,1)S(1)}, u32[]{:S(2)}, u32[]{:S(2)}) collective-permute-start(bf16[2,1024,128]{2,1,0:T(8,128)(2,1)S(1)} %get-tuple-element.32.q_ref), channel_id=1, source_target_pairs={{0,3},{1,2},{2,1},{3,0},{4,7},{5,6},{6,5},{7,4},{8,11},{9,10},{10,... | collective-permute-start | bytes 1572872 | tf_op jit(solution)/shard_map/ppermute | solution.py:251
  25.3 26.6 %collective-permute-start.2 = (bf16[2,1024,128]{2,1,0:T(8,128)(2,1)S(1)}, bf16[2,1024,128]{2,1,0:T(8,128)(2,1)S(1)}, u32[]{:S(2)}, u32[]{:S(2)}) collective-permute-start(bf16[2,1024,128]{2,1,0:T(8,128)(2,1)S(1)} %get-tuple-element.32.q_ref), channel_id=1, source_target_pairs={{0,2},{1,3},{2,0},{3,1},{4,6},{5,7},{6,4},{7,5},{8,10},{9,11},{10,... | collective-permute-start | bytes 1572872 | tf_op jit(solution)/shard_map/ppermute | solution.py:251
  25.8 22.9 %collective-permute-start = (bf16[2,1024,128]{2,1,0:T(8,128)(2,1)S(1)}, bf16[2,1024,128]{2,1,0:T(8,128)(2,1)S(1)}, u32[]{:S(2)}, u32[]{:S(2)}) collective-permute-start(bf16[2,1024,128]{2,1,0:T(8,128)(2,1)S(1)} %get-tuple-element.32.q_ref), channel_id=1, source_target_pairs={{0,1},{1,0},{2,3},{3,2},{4,5},{5,4},{6,7},{7,6},{8,9},{9,8},{10,11... | collective-permute-start | bytes 1572872 | tf_op jit(solution)/shard_map/ppermute | solution.py:251
  48.8 3.1 %copy-start.13 = (bf16[2,1024,128]{2,1,0:T(8,128)(2,1)}, bf16[2,1024,128]{2,1,0:T(8,128)(2,1)S(1)}, u32[]{:S(2)}) copy-start(bf16[2,1024,128]{2,1,0:T(8,128)(2,1)S(1)} %collective-permute-done.q_ref) | copy-start | bytes 1572868
  48.8 1.2 %copy-start.21 = (bf16[256,1024]{1,0:T(8,128)(2,1)S(1)}, bf16[256,1024]{1,0:T(8,128)(2,1)}, u32[]{:S(2)}) copy-start(bf16[256,1024]{1,0:T(8,128)(2,1)} %copy-done.20) | copy-start | bytes 1572868
  50.0 1.0 copy-start.24
  51.9 0.8 copy-start.10
  52.7 1.0 copy-start.11
  54.6 0.8 copy-start.7
  55.4 1.0 copy-start.8
  59.6 2.2 %copy-start.15 = (bf16[2048,1024]{1,0:T(8,128)(2,1)S(1)}, bf16[2048,1024]{1,0:T(8,128)(2,1)}, u32[]{:S(2)}) copy-start(bf16[2048,1024]{1,0:T(8,128)(2,1)} %all-gather.2.cloned.1.call-done.x_ref) | copy-start | bytes 12582916
  61.8 1.6 %copy-start.17 = (bf16[1024,1024]{1,0:T(8,128)(2,1)S(1)}, bf16[1024,1024]{1,0:T(8,128)(2,1)}, u32[]{:S(2)}) copy-start(bf16[1024,1024]{1,0:T(8,128)(2,1)} %copy-done.16) | copy-start | bytes 6291460
  63.4 1.6 %copy-start.19 = (bf16[1024,1024]{1,0:T(8,128)(2,1)S(1)}, bf16[1024,1024]{1,0:T(8,128)(2,1)}, u32[]{:S(2)}) copy-start(bf16[1024,1024]{1,0:T(8,128)(2,1)} %copy-done.18) | copy-start | bytes 6291460
  65.0 9.1 %copy-start.14 = (bf16[2,1024,128]{2,1,0:T(8,128)(2,1)S(1)}, bf16[2,1024,128]{2,1,0:T(8,128)(2,1)}, u32[]{:S(2)}) copy-start(bf16[2,1024,128]{2,1,0:T(8,128)(2,1)} %copy-done.13) | copy-start | bytes 1572868
  74.0 5.2 %copy-start.12 = (bf16[2,1024,128]{2,1,0:T(8,128)(2,1)S(1)}, bf16[2,1024,128]{2,1,0:T(8,128)(2,1)}, u32[]{:S(2)}) copy-start(bf16[2,1024,128]{2,1,0:T(8,128)(2,1)} %copy-done.10) | copy-start | bytes 1572868
  77.1 31.4 %collective-permute-start.1 = (bf16[2,1024,128]{2,1,0:T(8,128)(2,1)S(1)}, bf16[2,1024,128]{2,1,0:T(8,128)(2,1)S(1)}, u32[]{:S(2)}, u32[]{:S(2)}) collective-permute-start(bf16[2,1024,128]{2,1,0:T(8,128)(2,1)S(1)} %get-tuple-element.46), channel_id=1, source_target_pairs={{0,1},{1,0},{2,3},{3,2},{4,5},{5,4},{6,7},{7,6},{8,9},{9,8},{10,11... | collective-permute-start | bytes 1572872 | tf_op jit(solution)/shard_map/ppermute | solution.py:251
  79.3 3.6 %copy-start.9 = (bf16[2,1024,128]{2,1,0:T(8,128)(2,1)S(1)}, bf16[2,1024,128]{2,1,0:T(8,128)(2,1)}, u32[]{:S(2)}) copy-start(bf16[2,1024,128]{2,1,0:T(8,128)(2,1)} %copy-done.7) | copy-start | bytes 1572868
  80.6 27.9 %collective-permute-start.3 = (bf16[2,1024,128]{2,1,0:T(8,128)(2,1)S(1)}, bf16[2,1024,128]{2,1,0:T(8,128)(2,1)S(1)}, u32[]{:S(2)}, u32[]{:S(2)}) collective-permute-start(bf16[2,1024,128]{2,1,0:T(8,128)(2,1)S(1)} %get-tuple-element.50), channel_id=1, source_target_pairs={{0,2},{1,3},{2,0},{3,1},{4,6},{5,7},{6,4},{7,5},{8,10},{9,11},{10,... | collective-permute-start | bytes 1572872 | tf_op jit(solution)/shard_map/ppermute | solution.py:251
  82.9 5.2 %copy-start.6 = (bf16[2,1024,128]{2,1,0:T(8,128)(2,1)S(1)}, bf16[2,1024,128]{2,1,0:T(8,128)(2,1)}, u32[]{:S(2)}) copy-start(bf16[2,1024,128]{2,1,0:T(8,128)(2,1)} %copy-done.5) | copy-start | bytes 1572868
  82.9 5.2 %copy-start.22 = (bf16[256,1024]{1,0:T(8,128)(2,1)S(1)}, bf16[256,1024]{1,0:T(8,128)(2,1)}, u32[]{:S(2)}) copy-start(bf16[256,1024]{1,0:T(8,128)(2,1)} %copy-done.20) | copy-start | bytes 1572868
  82.9 5.2 %copy-start.25 = (bf16[2,1024,128]{2,1,0:T(8,128)(2,1)S(1)}, bf16[2,1024,128]{2,1,0:T(8,128)(2,1)}, u32[]{:S(2)}) copy-start(bf16[2,1024,128]{2,1,0:T(8,128)(2,1)} %copy-done.23) | copy-start | bytes 1572868
  85.4 23.1 %collective-permute-start.5 = (bf16[2,1024,128]{2,1,0:T(8,128)(2,1)S(1)}, bf16[2,1024,128]{2,1,0:T(8,128)(2,1)S(1)}, u32[]{:S(2)}, u32[]{:S(2)}) collective-permute-start(bf16[2,1024,128]{2,1,0:T(8,128)(2,1)S(1)} %get-tuple-element.54), channel_id=1, source_target_pairs={{0,3},{1,2},{2,1},{3,0},{4,7},{5,6},{6,5},{7,4},{8,11},{9,10},{10,... | collective-permute-start | bytes 1572872 | tf_op jit(solution)/shard_map/ppermute | solution.py:251
  86.5 17.2 %collective-permute-start.6 = (f32[2,2,8,256]{3,2,1,0:T(8,128)S(1)}, f32[2,2,8,256]{3,2,1,0:T(8,128)S(1)}, u32[]{:S(2)}, u32[]{:S(2)}) collective-permute-start(f32[2,2,8,256]{3,2,1,0:T(8,128)S(1)} %get-tuple-element.56), channel_id=1, source_target_pairs={{0,1},{1,0},{2,3},{3,2},{4,5},{5,4},{6,7},{7,6},{8,9},{9,8},{10,11... | collective-permute-start | bytes 98312 | tf_op jit(solution)/shard_map/ppermute | solution.py:251
  91.3 16.3 %collective-permute-start.7 = (f32[2,2,8,256]{3,2,1,0:T(8,128)S(1)}, f32[2,2,8,256]{3,2,1,0:T(8,128)S(1)}, u32[]{:S(2)}, u32[]{:S(2)}) collective-permute-start(f32[2,2,8,256]{3,2,1,0:T(8,128)S(1)} %get-tuple-element.57), channel_id=1, source_target_pairs={{0,2},{1,3},{2,0},{3,1},{4,6},{5,7},{6,4},{7,5},{8,10},{9,11},{10,... | collective-permute-start | bytes 98312 | tf_op jit(solution)/shard_map/ppermute | solution.py:251
  103.7 4.8 %collective-permute-start.8 = (f32[2,2,8,256]{3,2,1,0:T(8,128)S(1)}, f32[2,2,8,256]{3,2,1,0:T(8,128)S(1)}, u32[]{:S(2)}, u32[]{:S(2)}) collective-permute-start(f32[2,2,8,256]{3,2,1,0:T(8,128)S(1)} %get-tuple-element.58), channel_id=1, source_target_pairs={{0,3},{1,2},{2,1},{3,0},{4,7},{5,6},{6,5},{7,4},{8,11},{9,10},{10,... | collective-permute-start | bytes 98312 | tf_op jit(solution)/shard_map/ppermute | solution.py:251
  103.7 4.8 %copy-start.3 = (bf16[256,1024]{1,0:T(8,128)(2,1)S(1)}, bf16[256,1024]{1,0:T(8,128)(2,1)}, u32[]{:S(2)}) copy-start(bf16[256,1024]{1,0:T(8,128)(2,1)} %refs_0_.1) | copy-start | bytes 1572868
  103.7 4.8 %copy-start.4 = (bf16[1024,1024]{1,0:T(8,128)(2,1)S(1)}, bf16[1024,1024]{1,0:T(8,128)(2,1)}, u32[]{:S(2)}) copy-start(bf16[1024,1024]{1,0:T(8,128)(2,1)} %refs_1_.1) | copy-start | bytes 6291460
Sparse Core Ops, SparseCore 0:
  8.9 49.5 all-gather.1
